TPU v7x, 32 devices: a whole 2x2x4 slice. The times are simulated.
32 devices in a mesh: dp: 8 (over y, x, core), tensor: 4 (over z).
Axes of the slice: x: 2, y: 2, z: 4, core: 2. Of those that a mesh axis runs over, the one named last changes fastest.
Arguments:
- layer_input: bfloat16 [4096, 2048], P(('dp', 'tensor')), may hold values from -6 to 6
- segment_ids: int32 [4096], P('dp'), may hold values from 0 to 15, as said below
- norm_attn: bfloat16 [2048], P('dp'), may hold values from 0.5 to 1.5
- w_query: bfloat16 [2048, 2048], P('dp', 'tensor')
- w_key: bfloat16 [2048, 256], P('dp', 'tensor')
- w_value: bfloat16 [2048, 256], P('dp', 'tensor'), may hold values from -0.125 to 0.125
- w_output: bfloat16 [2048, 2048], P('tensor', 'dp'), may hold values from -0.5 to 0.5
- norm_ffn: bfloat16 [2048], P('dp'), may hold values from 0.5 to 1.5
- w_gate: bfloat16 [2048, 5632], P('dp', 'tensor'), may hold values from -0.125 to 0.125
- w_up: bfloat16 [2048, 5632], P('dp', 'tensor'), may hold values from -0.125 to 0.125
- w_down: bfloat16 [5632, 2048], P('tensor', 'dp'), may hold values from -0.078125 to 0.078125
- cotangent: bfloat16 [4096, 2048], P(('dp', 'tensor')), may hold values from -6 to 6
Outputs:
- layer_output: bfloat16 [4096, 2048], P(('dp', 'tensor'))
- grad_input: float32 [4096, 2048], P(('dp', 'tensor'))
- grad_norm_attn: float32 [2048], P('dp')
- grad_w_query: float32 [2048, 2048], P('dp', 'tensor')
- grad_w_key: float32 [2048, 256], P('dp', 'tensor')
- grad_w_value: float32 [2048, 256], P('dp', 'tensor')
- grad_w_output: float32 [2048, 2048], P('tensor', 'dp')
- grad_norm_ffn: float32 [2048], P('dp')
- grad_w_gate: float32 [2048, 5632], P('dp', 'tensor')
- grad_w_up: float32 [2048, 5632], P('dp', 'tensor')
- grad_w_down: float32 [5632, 2048], P('tensor', 'dp')
Inputs may be any that keep to these rules, and one draw needn't show every extreme that they name: `segment_ids`: within each aligned block of 512 rows the ids start at 0, never fall and rise by one at each new sequence, so that a block holds 1 to 16 sequences; in every draw some block is a single sequence of 512 rows and some block holds 16.
All inputs are finite; a program needn't handle non-finite values.
Results may differ from a plain program's by a relative error of at most 0.014.
Values may be sent and summed in bfloat16 or wider, within the bound.
A program may use at most 192 MiB of HBM per device.

v0:
```python
import functools
import math

import jax
import jax.numpy as jnp
from jax import lax
from jax.experimental import pallas as pl
from jax.experimental.pallas import tpu as pltpu
from jax.sharding import PartitionSpec as P

HD = 64
EPSILON = 1e-05
NEGATIVE = -1e30
LANES = 128
BF = jnp.bfloat16
F32 = jnp.float32
VMEM_BYTES = 67_000_000


def spans(bits):
    masks = [0]
    for bit in bits:
        masks = masks + [mask | (1 << bit) for mask in masks]
    return masks


def flip(index, mask, width):
    total = 0
    for bit in range(width):
        own = lax.rem(lax.div(index, 1 << bit), 2)
        if isinstance(mask, int):
            other = (mask >> bit) & 1
        else:
            other = lax.rem(lax.div(mask, 1 << bit), 2)
        total = total + lax.rem(own + other, 2) * (1 << bit)
    return total


def aligned(value, step):
    return value if isinstance(value, int) else pl.multiple_of(value, step)


def remote(src, dst, send_sem, recv_sem, device):
    return pltpu.make_async_remote_copy(
        src_ref=src,
        dst_ref=dst,
        send_sem=send_sem,
        recv_sem=recv_sem,
        device_id=device,
        device_id_type=pl.DeviceIdType.MESH,
    )


def dot(left, right, left_dim=1, right_dim=0):
    return lax.dot_general(
        left, right, (((left_dim,), (right_dim,)), ((), ())), preferred_element_type=F32
    )


def tiles_of(size, most):
    units = size // LANES
    parts = -(-units // most)
    cuts, start = [], 0
    for part in range(parts):
        width = (units // parts + (1 if part < units % parts else 0)) * LANES
        cuts.append((start, width))
        start += width
    return cuts


def over_cols(size, width, body):
    @pl.loop(0, size // width)
    def _(i):
        body(pl.ds(pl.multiple_of(i * width, width), width))


def enter(t, nt, me, width, barrier, everyone_along_tensor=False):
    signal = functools.partial(
        pl.semaphore_signal, barrier, inc=1, device_id_type=pl.DeviceIdType.MESH
    )
    for mask in range(1, 1 << width):
        signal(device_id={"dp": flip(me, mask, width)})
    if everyone_along_tensor:
        for step in range(1, nt):
            signal(device_id={"tensor": lax.rem(t + step, nt)})
        pl.semaphore_wait(barrier, (1 << width) - 1 + nt - 1)
        return

    @pl.when(t > 0)
    def _():
        signal(device_id={"tensor": t - 1})

    @pl.when(t < nt - 1)
    def _():
        signal(device_id={"tensor": t + 1})

    neighbours = lax.min(t, 1) + lax.min(nt - 1 - t, 1)
    pl.semaphore_wait(barrier, (1 << width) - 1 + neighbours)


class LineGather:
    def __init__(self, full, row, size, t, nt, sems):
        self.full, self.row, self.size = full, row, size
        self.t, self.nt, self.sems = t, nt, sems
        self.pieces = sems.shape[2]
        self.done = set()

    def window(self, j, s):
        return self.full.at[pl.ds(aligned(self.row(j, s), self.size), self.size), :]

    def right(self, j, s):
        at = self.window(j, s)
        return remote(
            at, at, self.sems.at[0, j, s], self.sems.at[2, j, s],
            {"tensor": lax.rem(self.t + 1, self.nt)},
        )

    def left(self, j, s):
        at = self.window(j, s)
        return remote(
            at, at, self.sems.at[1, j, s], self.sems.at[3, j, s],
            {"tensor": lax.rem(self.t + self.nt - 1, self.nt)},
        )

    def start(self, s):
        @pl.when(self.t < self.nt - 1)
        def _():
            self.right(self.t, s).start()

        @pl.when(self.t > 0)
        def _():
            self.left(self.t, s).start()

    def step(self, k, s):
        t, nt = self.t, self.nt
        if k >= nt or (k, s) in self.done:
            return
        self.done.add((k, s))

        @pl.when(t >= k)
        def _():
            self.right(t - k, s).wait_recv()

            @pl.when(t < nt - 1)
            def _():
                self.right(t - k, s).start()

        @pl.when(t + k < nt)
        def _():
            self.left(t + k, s).wait_recv()

            @pl.when(t > 0)
            def _():
                self.left(t + k, s).start()

    def complete(self, pieces):
        for k in range(1, self.nt):
            for s in pieces:
                self.step(k, s)

    def finish(self, pieces):
        t, nt = self.t, self.nt

        @pl.loop(0, nt)
        def _(k):
            for s in pieces:
                @pl.when((t >= k) & (t < nt - 1))
                def _():
                    self.right(t - k, s).wait_send()

                @pl.when((t + k < nt) & (t > 0))
                def _():
                    self.left(t + k, s).wait_send()


class LineScatter:
    def __init__(self, part, row, sent, arrived, t, nt, sems):
        self.part, self.row, self.sent, self.arrived = part, row, sent, arrived
        self.t, self.nt, self.sems = t, nt, sems
        self.pieces = sems.shape[3]
        self.size = sent.shape[1] // self.pieces
        self.model = sent.shape[2]
        self.near = lax.div(2 * t, nt)
        self.far = 1 - self.near

    def sub(self, s):
        return pl.ds(s * self.size, self.size)

    def depth(self, way):
        return (1 - way) * self.t + way * (self.nt - 1 - self.t)

    def goal(self, way, i):
        return (1 - way) * (self.nt - 1 - i) + way * i

    def slot(self, way, j):
        return j + 1 - way

    def move(self, way, j, s):
        return remote(
            self.sent.at[j, self.sub(s), :], self.arrived.at[self.slot(way, j), self.sub(s), :],
            self.sems.at[0, way, j, s], self.sems.at[1, way, j, s],
            {"tensor": lax.rem(self.t + self.nt + 1 - 2 * way, self.nt)},
        )

    def rows(self, j, s):
        return pl.ds(aligned(self.row(j, s), self.size), self.size)

    def mine(self, j, s):
        return self.part[self.rows(j, s), : self.model]

    def edge(self, s):
        t, nt = self.t, self.nt

        @pl.when((t == 0) | (t == nt - 1))
        def _():
            way = lax.div(t, nt - 1)

            @pl.loop(0, nt - 1)
            def _(i):
                j = self.goal(way, i)
                self.sent[j, self.sub(s), :] = self.mine(j, s).astype(BF)
                self.move(way, j, s).start()

    def relay(self, way, s):
        depth = self.depth(way)

        @pl.when(depth > 0)
        def _():
            @pl.loop(0, self.nt - 1 - depth)
            def _(i):
                j = self.goal(way, i)
                self.move(way, j, s).wait_recv()
                total = self.mine(j, s) + self.arrived[self.slot(way, j), self.sub(s), :].astype(F32)
                self.sent[j, self.sub(s), :] = total.astype(BF)
                self.move(way, j, s).start()

    def own(self, s):
        t = self.t
        rows = self.rows(t, s)
        for way in (self.near, self.far):
            @pl.when(self.depth(way) > 0)
            def _():
                self.move(way, t, s).wait_recv()
                self.part[rows, : self.model] += self.arrived[self.slot(way, t), self.sub(s), :].astype(F32)

        return rows

    def finish(self, pieces):
        for way in range(2):
            @pl.loop(0, self.nt - 1 - self.depth(way))
            def _(i):
                for s in pieces:
                    self.move(way, self.goal(way, i), s).wait_send()


class Cube:
    def setup(self, me, width, half_send, half_recv, pair_send, pair_recv):
        self.me, self.width = me, width
        self.hs, self.hr, self.ps, self.pr = half_send, half_recv, pair_send, pair_recv
        self.bits = list(range(1, width))
        self.orders = (self.bits, self.bits[::-1])
        self.masks = spans(self.bits)
        self.stages = len(self.bits)

    def at(self, mask):
        return flip(self.me, mask, self.width)


class BlockGather(Cube):
    def __init__(self, own, full, by_rows, me, width, *sems):
        self.setup(me, width, *sems)
        self.own_ref, self.full, self.by_rows = own, full, by_rows

    def half(self, h):
        rows = self.own_ref.shape[0] // 2
        return self.own_ref.at[pl.ds(h * rows, rows), :]

    def window(self, who, h=None):
        rows, cols = self.own_ref.shape
        take, start = (rows, 0) if h is None else (rows // 2, h * (rows // 2))
        if self.by_rows:
            return self.full.at[pl.ds(aligned(who * rows + start, take), take), :]
        return self.full.at[pl.ds(start, take), pl.ds(aligned(who * cols, cols), cols)]

    def hop(self, stage, h, m):
        order = self.orders[h]
        bit = 1 << order[stage]
        slot = (m | bit) >> 1
        src = self.half(h) if m == 0 else self.window(self.at(m), h)
        return remote(
            src, self.window(self.at(m), h), self.hs.at[h, slot - 1], self.hr.at[h, slot - 1],
            {"dp": self.at(bit)},
        )

    def send(self, stage):
        for h in range(2):
            for m in spans(self.orders[h][:stage]):
                self.hop(stage, h, m).start()

    def wait(self, stage):
        for h in range(2):
            bit = 1 << self.orders[h][stage]
            for m in spans(self.orders[h][:stage]):
                slot = (m | bit) >> 1
                landed = self.window(self.at(m | bit), h)
                remote(
                    landed, landed, self.hs.at[h, slot - 1], self.hr.at[h, slot - 1],
                    {"dp": self.at(bit)},
                ).wait_recv()

    def pair(self, m):
        src = self.own_ref if m == 0 else self.window(self.at(m))
        return remote(
            src, self.window(self.at(m)), self.ps.at[m >> 1], self.pr.at[m >> 1],
            {"dp": self.at(1)},
        )

    def pair_own(self):
        self.pair(0).start()

    def pair_send(self):
        for m in self.masks:
            if m:
                self.pair(m).start()

    def pair_wait(self):
        for m in self.masks:
            landed = self.window(self.at(m | 1))
            remote(
                landed, landed, self.ps.at[m >> 1], self.pr.at[m >> 1], {"dp": self.at(1)}
            ).wait_recv()

    def place(self, sem):
        return pltpu.make_async_copy(self.own_ref, self.window(self.me), sem)

    def drain(self):
        for stage in range(self.stages):
            for h in range(2):
                for m in spans(self.orders[h][:stage]):
                    self.hop(stage, h, m).wait_send()
        for m in self.masks:
            self.pair(m).wait_send()


class BlockScatter(Cube):
    def __init__(self, chunk, out_sent, total, landed, store, me, width, *sems):
        self.setup(me, width, *sems)
        self.chunk, self.sent, self.total, self.landed = chunk, out_sent, total, landed
        self.store = store
        self.slots = 1 << (width - 1)

    def pair(self, slot):
        return remote(
            self.sent.at[slot], self.total.at[slot], self.ps.at[slot], self.pr.at[slot],
            {"dp": self.at(1)},
        )

    def give(self):
        @pl.loop(0, self.slots)
        def _(k):
            slot = self.slots - 1 - k
            self.sent[slot] = self.chunk(self.at(2 * slot + 1)).astype(BF)
            self.pair(slot).start()

    def given(self):
        @pl.loop(0, self.slots)
        def _(slot):
            self.pair(slot).wait_send()

    def take(self):
        @pl.loop(0, self.slots)
        def _(k):
            slot = self.slots - 1 - k
            term = self.chunk(self.at(2 * slot))
            self.pair(slot).wait_recv()
            self.total[slot] = (term + self.total[slot].astype(F32)).astype(BF)

    def moves(self, stage):
        for h in range(2):
            order = self.orders[h]
            last = self.stages - 1 - stage
            bit = 1 << order[last]
            for m in spans(order[:last]):
                yield h, bit, m | bit

    def hop(self, h, bit, m):
        rows = self.total.shape[1] // 2
        return remote(
            self.total.at[m >> 1, pl.ds(h * rows, rows), :], self.landed.at[h, (m >> 1) - 1],
            self.hs.at[h, (m >> 1) - 1], self.hr.at[h, (m >> 1) - 1], {"dp": self.at(bit)},
        )

    def send(self, stage):
        for h, bit, m in self.moves(stage):
            self.hop(h, bit, m).start()

    def add(self, stage):
        rows = self.total.shape[1] // 2
        for h, bit, m in self.moves(stage):
            self.hop(h, bit, m).wait_recv()
            keep = (m ^ bit) >> 1
            at = slice(h * rows, (h + 1) * rows)
            total = self.total[keep, at, :].astype(F32) + self.landed[h, (m >> 1) - 1].astype(F32)
            if stage == self.stages - 1:
                self.store(at, total)
            else:
                self.total[keep, at, :] = total.astype(BF)

    def drain(self):
        for stage in range(self.stages):
            for h, bit, m in self.moves(stage):
                self.hop(h, bit, m).wait_send()


def inverse_of(rows):
    return lax.rsqrt(jnp.mean(rows * rows, axis=-1, keepdims=True) + EPSILON)


def times_gain(unit, gains, which, store):
    parts, _, width = gains.shape
    for d in range(parts):
        cols = slice(d * width, (d + 1) * width)
        store(cols, unit[:, cols] * gains[d, which : which + 1, :])


def lane_index(shape):
    return lax.broadcasted_iota(jnp.int32, shape, len(shape) - 1)


def column_of(segr):
    rows = segr.shape[1]
    wide = jnp.broadcast_to(segr[...].astype(F32), (8, rows))
    return jnp.transpose(wide)[:, 0:1]


def rope_into(cos_ref, sin_ref, segr):
    rows = segr.shape[1]
    before = (segr[...].astype(F32) < column_of(segr)).astype(F32)
    start = jnp.sum(before, axis=1, keepdims=True)
    position = lax.broadcasted_iota(jnp.int32, (rows, 1), 0).astype(F32) - start
    lane = lane_index((rows, LANES))
    half = HD // 2
    frequency = jnp.exp(lax.rem(lane, half).astype(F32) * (-math.log(10000.0) / half))
    angle = position * frequency
    cos_ref[...] = jnp.cos(angle)
    sine = jnp.sin(angle)
    sin_ref[...] = jnp.where(lax.rem(lane, HD) < half, -sine, sine)


def swapped(x):
    lane = lane_index(x.shape)
    half = HD // 2
    return jnp.where(
        lax.rem(lane, HD) < half,
        pltpu.roll(x, LANES - half, 1),
        pltpu.roll(x, half, 1),
    )


def bias_into(bias, segr):
    rows = segr.shape[1]
    query = lax.broadcasted_iota(jnp.int32, (rows, rows), 0)
    key = lax.broadcasted_iota(jnp.int32, (rows, rows), 1)
    seen = (segr[...].astype(F32) == column_of(segr)) & (query >= key)
    bias[...] = jnp.where(seen, 0.0, NEGATIVE)


def pad_pair(keys_values, keys, values):
    low = lane_index(keys_values.shape) < HD
    key = jnp.where(low, keys_values, 0.0)
    value = jnp.where(low, 0.0, keys_values)
    keys[0] = key.astype(BF)
    keys[1] = pltpu.roll(key, HD, 1).astype(BF)
    values[0] = pltpu.roll(value, HD, 1).astype(BF)
    values[1] = value.astype(BF)


def query_cuts(rows):
    block = 256 if rows % 256 == 0 else rows
    return [(start, block, start + block) for start in range(0, rows, block)]


def attend_pairs(first, last, qo, kpad, vpad, bias, mo, lo):
    rows = qo.shape[0]
    lane = lane_index((1, LANES))

    @pl.loop(first, last)
    def _(pair):
        lanes = pl.ds(pl.multiple_of(pair * LANES, LANES), LANES)
        for start, block, seen in query_cuts(rows):
            at = slice(start, start + block)
            query = qo[at, lanes]
            mixed = jnp.zeros((block, LANES), F32)
            logs = lo[at, :]
            for side in range(2):
                scores = dot(query, kpad[side, :seen, :], 1, 1) + bias[at, :seen]
                top = jnp.max(scores, axis=-1, keepdims=True)
                probs = jnp.exp(scores - top)
                total = jnp.sum(probs, axis=-1, keepdims=True)
                mixed = mixed + dot(probs.astype(BF), vpad[side, :seen, :]) / total
                logs = jnp.where(lane == 2 * pair + side, top + jnp.log(total), logs)
            lo[at, :] = logs
            mo[at, lanes] = mixed.astype(BF)


def back_through_norm(raw, grads, gains, which, store, store_gain):
    parts, _, width = gains.shape
    cuts = [slice(d * width, (d + 1) * width) for d in range(parts)]
    model = parts * width
    square = sum(jnp.sum(raw(c) * raw(c), axis=-1, keepdims=True) for c in cuts)
    inverse = lax.rsqrt(square / model + EPSILON)
    mean = 0.0
    for d, c in enumerate(cuts):
        unit = raw(c) * inverse
        grad = grads(c)
        store_gain(c, jnp.sum(grad * unit, axis=0, keepdims=True))
        mean = mean + jnp.sum(grad * gains[d, which : which + 1, :] * unit, axis=-1, keepdims=True)
    mean = mean / model
    for d, c in enumerate(cuts):
        unit = raw(c) * inverse
        store(c, inverse * (grads(c) * gains[d, which : which + 1, :] - unit * mean))


def attend_back_pairs(first, last, qo, gm, mo, lo, kpad, vpad, bias, cos, sin, dqkv, dkey, dval):
    rows = qo.shape[0]

    @pl.loop(first, last)
    def _(pair):
        lanes = pl.ds(pl.multiple_of(pair * LANES, LANES), LANES)
        for start, block, seen in query_cuts(rows):
            at = slice(start, start + block)
            lane = lane_index((block, LANES))
            query, grad = qo[at, lanes], gm[at, lanes]
            both = grad.astype(F32) * mo[at, lanes].astype(F32)
            logs = lo[at, :]
            dq = jnp.zeros((block, LANES), F32)
            for side in range(2):
                inside = (lane >= HD) if side else (lane < HD)
                delta = jnp.sum(jnp.where(inside, both, 0.0), axis=-1, keepdims=True)
                log = jnp.sum(
                    jnp.where(lane == 2 * pair + side, logs, 0.0), axis=-1, keepdims=True
                )
                key, value = kpad[side, :seen, :], vpad[side, :seen, :]
                probs = jnp.exp(dot(query, key, 1, 1) + bias[at, :seen] - log)
                grad_scores = (probs * (dot(grad, value, 1, 1) - delta)).astype(BF)
                dq = dq + dot(grad_scores, key)
                dkey[side, :seen, :] += dot(grad_scores, query, 0, 0)
                dval[side, :seen, :] += dot(probs.astype(BF), grad, 0, 0)
            dq = dq * HD ** (-0.5)
            dqkv[at, lanes] = (dq * cos[at, :] - swapped(dq) * sin[at, :]).astype(BF)


PIECES = 4


def vmem():
    return pl.BlockSpec(memory_space=pltpu.VMEM)


def hbm():
    return pl.BlockSpec(memory_space=pl.ANY)


def dma(*shape):
    return pltpu.SemaphoreType.DMA(shape)


def line_scratch(nt, rows, model):
    return [pltpu.VMEM((nt, rows, model), BF), pltpu.VMEM((nt + 1, rows, model), BF)]


def ticks(pieces, nt):
    return [
        [(k, tick - k) for k in range(1, nt) if 0 <= tick - k < pieces]
        for tick in range(pieces + nt - 1)
    ]


def layer_kernel(
    nt, width,
    x, cot, gain_a, gain_f, segr, wq, wkt, wvt, wo, gate, up, down,
    y_o, gi_o, gain_o, d_wq_o, d_kv_o, d_wo_o, d_down_o, d_gate, d_up, wqkv_f, wo_f, na_f,
    rowsbuf, cf, branch, act, hid, gate_v, up_v, down_v, part, sent, arrived, totals, landed, stage_v,
    y, gi, gain_out, d_wq, d_kv, d_wo, d_down,
    own_qkv, gain, gall, qo, kvo, mo, lo, cos, sin, gsum, zslots, dslots,
    gain_sem, place_sem, out_sem, line_sem, cot_sem, sum_sem,
    hs, hr, ps, pr, zsem, dsem, emit_sem, ready, calm,
):
    me, t = lax.axis_index("dp"), lax.axis_index("tensor")
    nd = 1 << width
    rows, model = x.shape
    tokens = nt * rows
    queries = wq.shape[1]
    hidden = gate.shape[1]
    shard = model >> width
    wide = own_qkv.shape[1]
    pieces = PIECES
    first_half = pieces // 2
    size = rows // pieces
    cut = 512 if model % 512 == 0 else LANES

    def natural(j, s):
        return j * rows + s * size

    def shuffled(j, s):
        return (s * nt + j) * size

    local = pl.ds(pl.multiple_of(t * rows, rows), rows)
    rowsbuf[local, :] = x[...]
    gain[...] = jnp.zeros_like(gain)
    gain[0:1, :] = gain_a[...].astype(F32).reshape(1, shard)
    gain[1:2, :] = gain_f[...].astype(F32).reshape(1, shard)
    own_qkv[:, :queries] = wq[...]
    turned = jnp.concatenate([wkt[...].astype(F32), wvt[...].astype(F32)], axis=0)
    own_qkv[:, queries:] = jnp.transpose(turned).astype(BF)
    with jax.named_scope("enter"):
        enter(t, nt, me, width, pltpu.get_barrier_semaphore())

    tokens_x = LineGather(rowsbuf, natural, size, t, nt, line_sem)
    for s in range(pieces):
        tokens_x.start(s)
    gathers = []
    for w, (own, full, by_rows) in enumerate(
        ((own_qkv, wqkv_f, True), (wo, wo_f, False), (gate, gate_v, True), (up, up_v, True), (down, down_v, False))
    ):
        gathers.append(
            BlockGather(own, full, by_rows, me, width, hs.at[w], hr.at[w], ps.at[w], pr.at[w])
        )
    g_qkv, g_out, g_gate, g_up, g_down = gathers
    stages = g_qkv.stages

    def gain_copy(mask):
        return remote(
            gain, gall.at[me], gain_sem.at[0, mask], gain_sem.at[1, mask],
            {"dp": flip(me, mask, width)},
        )

    for mask in range(1, nd):
        gain_copy(mask).start()
    for g in (g_qkv, g_out, g_gate):
        g.send(0)
    for w, g in enumerate(gathers):
        g.place(place_sem.at[w]).start()
    gall[me] = gain[...]

    def forward(g, stage):
        g.wait(stage)
        if stage == 0:
            g.pair_own()
        if stage + 1 < stages:
            g.send(stage + 1)
        else:
            g.pair_send()

    for s in range(pieces):
        cf[pl.ds(pl.multiple_of(shuffled(t, s), size), size), :] = cot[s * size : (s + 1) * size, :]
    cots = LineGather(cf, shuffled, size, t, nt, cot_sem)
    scatter_o = LineScatter(part, shuffled, sent, arrived, t, nt, sum_sem)

    def attention(na, wqkv_v, wo_v, bias, kpad, vpad):
        bias_into(bias, segr)
        rope_into(cos, sin, segr)
        lo[...] = jnp.zeros_like(lo)
        for mask in range(1, nd):
            slot = gall.at[flip(me, mask, width)]
            remote(
                slot, slot, gain_sem.at[0, mask], gain_sem.at[1, mask],
                {"dp": flip(me, mask, width)},
            ).wait_recv()

        def norm(j):
            @pl.loop(0, pieces)
            def _(s):
                these = pl.ds(pl.multiple_of(j * rows + s * size, size), size)
                value = rowsbuf[these, :].astype(F32)

                def store(cols, normed):
                    na[these, cols] = normed.astype(BF)

                times_gain(value * inverse_of(value), gall, 0, store)

        norm(t)
        for stage in range(stages - 1):
            forward(g_qkv, stage)
            forward(g_out, stage)
        fills = [
            lambda: (forward(g_gate, 0), g_up.send(0)),
            lambda: (forward(g_qkv, stages - 1), forward(g_out, stages - 1), g_down.send(0)),
        ]
        load = pltpu.make_async_copy(wqkv_f, wqkv_v, place_sem.at[5])
        load_out = pltpu.make_async_copy(wo_f, wo_v, place_sem.at[6])

        def fetch():
            g_qkv.place(place_sem.at[0]).wait()
            g_qkv.pair_wait()
            load.start()
            g_out.place(place_sem.at[1]).wait()
            g_out.pair_wait()
            load_out.start()

        for k in range(1, nt):
            if k == nt - 1:
                for fill in fills:
                    fill()
                fills = []
                with jax.named_scope("fetch"):
                    fetch()
            with jax.named_scope("x_step"):
                for s in range(pieces):
                    tokens_x.step(k, s)
            if k == nt - 1:
                for s in range(first_half):
                    cots.start(s)

            @pl.when(t >= k)
            def _():
                norm(t - k)

            @pl.when(t + k < nt)
            def _():
                norm(t + k)

            if fills:
                with jax.named_scope("x_fill"):
                    fills.pop(0)()
        keep = pltpu.make_async_copy(na, na_f, out_sem.at[0])
        keep.start()
        with jax.named_scope("wait_qkv"):
            load.wait()
        with jax.named_scope("qkv"):
            part[:, :wide] = dot(na[...], wqkv_v[...])
            c, s_ = cos[...], sin[...]
            for start in range(0, queries, LANES):
                lanes = slice(start, start + LANES)
                value = part[:, lanes]
                qo[:, lanes] = ((value * c + swapped(value) * s_) * HD ** (-0.5)).astype(BF)
            value = part[:, queries : queries + LANES]
            keyed = jnp.where(lane_index(value.shape) < HD, value * c + swapped(value) * s_, value)
            kvo[...] = keyed.astype(BF)
            pad_pair(keyed, kpad, vpad)
        pairs = queries // LANES
        with jax.named_scope("att"):
            attend_pairs(0, pairs, qo, kpad, vpad, bias, mo, lo)
        load_out.wait()
        with jax.named_scope("outproj"):
            mixed = jnp.concatenate(
                [
                    mo[natural(j, s) : natural(j, s) + size, :]
                    for s in range(pieces)
                    for j in range(nt)
                ],
                axis=0,
            )

            def project(cols):
                part[:tokens, cols] = dot(mixed, wo_v[:, cols])

            over_cols(model, cut, project)
        keep.wait()
        tokens_x.finish(range(pieces))

    pl.run_scoped(
        attention,
        pltpu.VMEM((tokens, model), BF),
        pltpu.VMEM((model, wide), BF),
        pltpu.VMEM((queries, model), BF),
        pltpu.VMEM((tokens, tokens), F32),
        pltpu.VMEM((2, tokens, LANES), BF),
        pltpu.VMEM((2, tokens, LANES), BF),
    )

    gather_nf = LineGather(rowsbuf, shuffled, size, t, nt, line_sem)

    def take_hidden(s):
        at = scatter_o.own(s)
        block = slice(s * size, (s + 1) * size)
        hidden_rows = x[block, :].astype(F32) + part[at, :model]
        hid[block, :] = hidden_rows
        there = pl.ds(pl.multiple_of(shuffled(t, s), size), size)

        def store(cols, normed):
            rowsbuf[there, cols] = normed.astype(BF)

        times_gain(hidden_rows * inverse_of(hidden_rows), gall, 1, store)
        gather_nf.start(s)

    def chunk_of(left, right):
        def chunk(d):
            return dot(left[:, pl.ds(pl.multiple_of(d * shard, shard), shard)], right[...], 0, 0)

        return chunk

    def cube(w, totals_, landed_, store):
        return BlockScatter(
            None, None, totals_, landed_, store, me, width, hs.at[w], hr.at[w], ps.at[w], pr.at[w]
        )

    def store_stage(at, value):
        stage_v[at, :] = value

    def store_down(at, value):
        d_down[:, at] = value.T

    def store_qkv(at, value):
        d_wq[at, :] = value[:, :queries]
        d_kv[:, at] = value[:, queries:].T

    def store_wo(at, value):
        d_wo[:, at] = value.T

    for_qkv, for_wo = pl.ds(0, wide), pl.ds(wide, queries)
    s_gate = cube(5, totals.at[0], landed.at[0], store_stage)
    s_up = cube(6, totals.at[1], landed.at[1], store_stage)
    s_down = cube(5, totals.at[0], landed.at[0], store_down)
    s_qkv = cube(6, totals.at[1, :, :, for_qkv], landed.at[1, :, :, :, for_qkv], store_qkv)
    s_out = cube(7, totals.at[1, :, :, for_wo], landed.at[1, :, :, :, for_wo], store_wo)

    def take(s):
        s.take()
        s.send(0)

    def on(s, stage):
        s.add(stage)
        if stage + 1 < stages:
            s.send(stage + 1)

    scatter_y = LineScatter(part, shuffled, sent, arrived, t, nt, sum_sem)
    scope = jax.named_scope
    emitted = []

    def emit(src, dst):
        emitted.append(pltpu.make_async_copy(src, dst, emit_sem.at[len(emitted)]))
        emitted[-1].start()

    def y_part(h):
        mine = slice(h * (tokens // 2), (h + 1) * (tokens // 2))
        with scope("y_part"):

            def product(cols):
                part[mine, cols] = dot(act[mine, :], down_v[:, cols])

            over_cols(model, cut, product)

    def y_near(s):
        with scope("y_near"):
            scatter_y.relay(scatter_y.near, s)

    def y_far(s):
        with scope("y_far"):
            scatter_y.relay(scatter_y.far, s)

    def y_own(s):
        with scope("y_own"):
            at = scatter_y.own(s)
            block_ = slice(s * size, (s + 1) * size)
            y[block_, :] = (hid[block_, :] + part[at, :model]).astype(BF)
            emit(y.at[pl.ds(s * size, size), :], y_o.at[pl.ds(s * size, size), :])

    def br(k, s):
        with scope("br_step"):
            gather_br.step(k, s)

    gsum[...] = jnp.zeros_like(gsum)
    gather_br = LineGather(branch, natural, size, t, nt, line_sem)

    def feed(dg, du, given):
        cuts = tiles_of(hidden, 6)
        span = max(width_ for _, width_ in cuts)
        half = tokens // 2
        block = 64

        def tile_in(h, i):
            start, width_ = cuts[i]
            at = slice(start, start + width_)
            held = mine = slice(h * half, (h + 1) * half)
            part[held, 0:width_] = dot(rowsbuf[mine, :], gate_v[:, at])
            part[held, span : span + width_] = dot(rowsbuf[mine, :], up_v[:, at])

        def tile_out(h, i):
            start, width_ = cuts[i]
            at = slice(start, start + width_)
            held = mine = slice(h * half, (h + 1) * half)
            part[held, 2 * span : 2 * span + width_] = dot(cf[mine, :], down_v[at, :], 1, 1)

            @pl.loop(0, half // block)
            def _(k):
                from_ = pl.ds(pl.multiple_of(h * half + k * block, block), block)
                to = pl.ds(pl.multiple_of(h * half + k * block, block), block)
                g = part[from_, 0:width_]
                u = part[from_, span : span + width_]
                ga = part[from_, 2 * span : 2 * span + width_]
                sig = 1.0 / (1.0 + jnp.exp(-g))
                gs = g * sig
                act[to, at] = (gs * u).astype(BF)
                du[to, at] = (ga * gs).astype(BF)
                dg[to, at] = (ga * u * sig * (1.0 + g * (1.0 - sig))).astype(BF)

        def tile(h, i):
            with scope("tile"):
                tile_in(h, i)
                tile_out(h, i)

        def back_dots(h):
            mine = slice(h * half, (h + 1) * half)

            def product(cols):
                part[mine, cols] = dot(dg[mine, :], gate_v[cols, :], 1, 1) + dot(
                    du[mine, :], up_v[cols, :], 1, 1
                )

            over_cols(model, cut, product)

        scatter_gn = LineScatter(part, shuffled, sent, arrived, t, nt, sum_sem)

        def take_grad(s):
            at = scatter_gn.own(s)
            block_ = slice(s * size, (s + 1) * size)
            there = pl.ds(pl.multiple_of(natural(t, s), size), size)

            def store(cols, value):
                total = cot[block_, cols].astype(F32) + value
                gi[block_, cols] = total
                branch[there, cols] = total.astype(BF)

            def store_gain(cols, value):
                gsum[1:2, cols] += value

            back_through_norm(
                lambda c: hid[block_, c], lambda c: part[at, c], gall, 1, store, store_gain
            )
            gather_br.start(s)

        s_gate.chunk, s_up.chunk = chunk_of(rowsbuf, dg), chunk_of(rowsbuf, du)
        s_gate.sent = s_up.sent = given

        half_a, half_b = range(first_half), range(first_half, pieces)
        def o_near(s):
            with scope("o_near"):
                scatter_o.relay(scatter_o.near, s)

        def o_far(s):
            with scope("o_far"):
                scatter_o.relay(scatter_o.far, s)

        def o_take(s):
            with scope("o_take"):
                take_hidden(s)

        def nf(k, s):
            with scope("nf_step"):
                gather_nf.step(k, s)

        def cot_steps(k, which):
            with scope("cot_step"):
                for s in which:
                    cots.step(k, s)

        def gn_near(s):
            with scope("gn_near"):
                scatter_gn.relay(scatter_gn.near, s)

        def gn_far(s):
            with scope("gn_far"):
                scatter_gn.relay(scatter_gn.far, s)

        def gn_take(s):
            with scope("gn_take"):
                take_grad(s)

        def weight(g, stage):
            with scope("weight"):
                if stage < stages:
                    forward(g, stage)

        scatter_o.edge(0)
        scatter_o.edge(1)
        cot_steps(1, half_a)
        weight(g_gate, 1)
        cot_steps(2, half_a)
        o_near(0)
        weight(g_up, 0)
        o_far(0)
        o_take(0)
        weight(g_down, 0)
        scatter_o.edge(2)
        o_near(1)
        o_far(1)
        nf(1, 0)
        cot_steps(3, half_a)
        o_take(1)
        scatter_o.edge(3)
        nf(1, 1)
        nf(2, 0)
        o_near(2)
        nf(2, 1)
        weight(g_up, 1)
        nf(3, 0)
        o_far(2)
        for s in half_b:
            cots.start(s)
        nf(3, 1)
        o_take(2)
        gather_nf.complete(half_a)
        cots.complete(half_a)
        weight(g_down, 1)
        for stage in range(2, stages):
            for g in (g_gate, g_up, g_down):
                weight(g, stage)
        o_near(3)
        with scope("wait_ffn"):
            for w in (2, 3):
                gathers[w].place(place_sem.at[w]).wait()
                gathers[w].pair_wait()
        with scope("tile"):
            tile_in(0, 0)
        with scope("wait_ffn"):
            g_down.place(place_sem.at[4]).wait()
            g_down.pair_wait()
        with scope("tile"):
            tile_out(0, 0)
        o_far(3)
        nf(1, 2)
        cot_steps(1, half_b)
        for i in range(1, len(cuts)):
            tile(0, i)
        o_take(3)
        nf(2, 2)
        with scope("back_dots"):
            scatter_o.finish(half_a)
            back_dots(0)
        scatter_gn.edge(0)
        scatter_gn.edge(1)
        nf(1, 3)
        cot_steps(2, half_b)
        gn_near(0)
        nf(3, 2)
        nf(2, 3)
        gn_far(0)
        cot_steps(3, half_b)
        gn_near(1)
        nf(3, 3)
        gather_nf.complete(half_b)
        cots.complete(half_b)
        gather_nf.finish(half_a)
        tile(1, 0)
        gn_far(1)
        gn_take(0)
        for i in range(1, len(cuts)):
            tile(1, i)
        with scope("back_dots"):
            scatter_o.finish(half_b)
            back_dots(1)
        scatter_gn.edge(2)
        gn_take(1)
        scatter_gn.edge(3)
        br(1, 0)
        with scope("gn_fill"):
            s_gate.give()
            br(2, 0)
            take(s_gate)
        gn_near(2)
        with scope("gn_fill"):
            s_gate.given()
            s_up.give()
        gn_far(2)
        br(1, 1)
        br(3, 0)
        with scope("gn_fill"):
            take(s_up)
        gn_near(3)
        gather_nf.finish(half_b)
        gn_take(2)
        y_part(0)
        scatter_gn.finish(half_a)
        scatter_y.edge(0)
        br(2, 1)
        gn_far(3)
        gn_take(3)
        scatter_y.edge(1)
        br(3, 1)
        br(1, 2)
        y_near(0)
        y_part(1)
        br(2, 2)
        br(1, 3)
        scatter_gn.finish(half_b)
        scatter_y.edge(2)
        scatter_y.edge(3)
        y_far(0)
        br(3, 2)
        br(2, 3)
        with scope("add0"):
            on(s_gate, 0)
        y_near(1)
        y_far(1)
        br(3, 3)
        gather_br.complete(range(pieces))
        s_up.given()

    pl.run_scoped(
        feed,
        pltpu.VMEM((tokens, hidden), BF),
        pltpu.VMEM((tokens, hidden), BF),
        pltpu.VMEM((nd // 2, shard, hidden), BF),
    )

    wo_v = down_v.at[pl.ds(0, queries), :]
    na_v = down_v.at[pl.ds(queries, tokens), :]
    wqkv_v = gate_v.at[:, pl.ds(0, wide)]
    gm = up_v.at[pl.ds(0, tokens), pl.ds(0, queries)]
    dqkv = up_v.at[pl.ds(tokens, tokens), pl.ds(0, wide)]

    def rear(bias, kpad, vpad, dkey, dval, given):
        inward = LineScatter(part, shuffled, sent, arrived, t, nt, sum_sem)
        for g in gathers:
            g.drain()
        loads = [
            pltpu.make_async_copy(wo_f, wo_v, place_sem.at[0]),
            pltpu.make_async_copy(wqkv_f, wqkv_v, place_sem.at[1]),
            pltpu.make_async_copy(na_f, na_v, place_sem.at[2]),
        ]
        for load in loads:
            load.start()
        bias_into(bias, segr)
        pad_pair(kvo[...].astype(F32), kpad, vpad)
        dkey[...] = jnp.zeros_like(dkey)
        dval[...] = jnp.zeros_like(dval)
        s_down.chunk, s_down.sent = chunk_of(cf, act), given
        s_qkv.chunk, s_qkv.sent = chunk_of(na_v, dqkv), given.at[:, :, for_qkv]
        s_out.chunk, s_out.sent = chunk_of(branch, mo), given.at[:, :, for_wo]

        def att(first, last):
            with scope("b_att"):
                attend_back_pairs(
                    first, last, qo, gm, mo, lo, kpad, vpad, bias, cos, sin, dqkv, dkey, dval
                )

        def free(s, out, slot):
            s.add(stages - 1)
            copy = pltpu.make_async_copy(stage_v, out, out_sem.at[1 + slot])
            copy.start()
            s.drain()
            for bit in range(width):
                pl.semaphore_signal(
                    ready.at[slot], inc=1, device_id={"dp": flip(me, 1 << bit, width)},
                    device_id_type=pl.DeviceIdType.MESH,
                )
            return copy

        def quiet(h):
            for step, there in ((-1, t > 0), (1, t < nt - 1)):
                @pl.when(there)
                def _():
                    pl.semaphore_signal(
                        calm.at[h], inc=1, device_id={"tensor": t + step},
                        device_id_type=pl.DeviceIdType.MESH,
                    )

        def gi_part(h):
            which = half_a if h == 0 else half_b
            mine = jnp.concatenate(
                [dqkv[natural(j, s) : natural(j, s) + size, :] for s in which for j in range(nt)],
                axis=0,
            )
            start_row = h * (tokens // 2)
            with scope("b_part"):

                def product(cols):
                    part[start_row : start_row + tokens // 2, cols] = dot(
                        mine, wqkv_v[cols, :], 1, 1
                    )

                over_cols(model, cut, product)
            with scope("calm"):
                pl.semaphore_wait(calm.at[h], lax.min(t, 1) + lax.min(nt - 1 - t, 1))
            for s in which:
                inward.edge(s)

        def gi_near(s):
            with scope("b_near"):
                inward.relay(inward.near, s)

        def gi_far(s):
            with scope("b_far"):
                inward.relay(inward.far, s)

        half_a, half_b = range(first_half), range(first_half, pieces)
        pairs = queries // LANES
        with scope("b_gm"):
            loads[0].wait()
            gm[...] = dot(branch[...], wo_v[...], 1, 1).astype(BF)
        for s in half_a:
            y_own(s)
        scatter_y.finish(half_a)
        quiet(0)
        with scope("add0"):
            on(s_up, 0)
        with scope("free0"):
            copy_gate = free(s_gate, d_gate, 0)

        @pl.loop(0, 2)
        def _(h):
            att(h * (pairs // 2), (h + 1) * (pairs // 2))

            @pl.when(h == 0)
            def _():
                y_near(2)

        with scope("b_give"):
            pl.semaphore_wait(ready.at[0], width)
            s_down.give()
        y_near(3)
        key = dkey[0] + pltpu.roll(dkey[1], HD, 1)
        value = pltpu.roll(dval[0], HD, 1) + dval[1]
        key = key * cos[...] - swapped(key) * sin[...]
        dqkv[:, queries : queries + LANES] = jnp.where(
            lane_index(key.shape) < HD, key, value
        ).astype(BF)
        loads[1].wait()
        gi_part(0)
        with scope("b_take"):
            take(s_down)
        y_far(2)
        with scope("free1"):
            copy_gate.wait()
            copies = [free(s_up, d_up, 1)]
        y_far(3)
        gi_near(0)
        with scope("b_fill"):
            loads[2].wait()
            s_down.given()
            pl.semaphore_wait(ready.at[1], width)
            s_qkv.give()
        for s in half_b:
            y_own(s)
        scatter_y.finish(half_b)
        quiet(1)
        gi_part(1)
        gi_far(0)
        with scope("b_fill"):
            take(s_qkv)
        gi_near(1)
        with scope("b_fill"):
            s_out.give()

        with scope("b_done"):
            for mask in range(1, nd):
                gain_copy(mask).wait_send()
            cots.finish(range(pieces))
            gather_br.finish(range(pieces))

        def take_grad(s):
            at = inward.own(s)
            block = slice(s * size, (s + 1) * size)

            def store(cols, value):
                gi[block, cols] += value

            def store_gain(cols, value):
                gsum[0:1, cols] += value

            back_through_norm(
                lambda c: x[block, c].astype(F32), lambda c: part[at, c], gall, 0, store, store_gain
            )

        fills = [
            functools.partial(on, s, stage)
            for stage in range(stages)
            for s in (s_down, s_qkv, s_out)
        ]
        gi_far(1)
        with scope("b_fill"):
            take(s_out)
        gi_near(2)
        gi_far(2)
        with scope("b_fill"):
            fills.pop(0)()
        gi_near(3)
        gi_far(3)
        with jax.named_scope("b_own"):
            for s in range(pieces):
                take_grad(s)
                emit(gi.at[pl.ds(s * size, size), :], gi_o.at[pl.ds(s * size, size), :])
                if s < pieces - 1 and fills:
                    fills.pop(0)()
        with jax.named_scope("b_gains"):
            zslots[t] = gsum[...]

            def along(step):
                return remote(
                    zslots.at[t], zslots.at[t], zsem.at[0, step], zsem.at[1, step],
                    {"tensor": lax.rem(t + step, nt)},
                )

            for step in range(1, nt):
                along(step).start()
        with jax.named_scope("b_gains"):
            for step in range(1, nt):
                slot = zslots.at[lax.rem(t + nt - step, nt)]
                remote(
                    slot, slot, zsem.at[0, step], zsem.at[1, step], {"tensor": lax.rem(t + step, nt)}
                ).wait_recv()
            gsum[...] = sum(zslots[i] for i in range(nt))

            def across(mask):
                peer = flip(me, mask, width)
                return remote(
                    gsum.at[:, pl.ds(pl.multiple_of(peer * shard, shard), shard)], dslots.at[me],
                    dsem.at[0, mask], dsem.at[1, mask], {"dp": peer},
                )

            for mask in range(1, nd):
                across(mask).start()
            dslots[me] = gsum[:, pl.ds(pl.multiple_of(me * shard, shard), shard)]
        with jax.named_scope("b_rest"):
            for fill in fills:
                fill()
            for src, dst in ((d_wq, d_wq_o), (d_kv, d_kv_o), (d_wo, d_wo_o), (d_down, d_down_o)):
                emit(src, dst)
        with jax.named_scope("b_gains"):
            for mask in range(1, nd):
                peer = flip(me, mask, width)
                slot = dslots.at[peer]
                remote(slot, slot, dsem.at[0, mask], dsem.at[1, mask], {"dp": peer}).wait_recv()
            gain_out[...] = sum(dslots[i] for i in range(nd))
            emit(gain_out, gain_o)
            for step in range(1, nt):
                along(step).wait_send()
            for mask in range(1, nd):
                across(mask).wait_send()
        with jax.named_scope("end"):
            for s in (s_qkv, s_out):
                s.given()
            for s in (s_down, s_qkv, s_out):
                s.drain()
            inward.finish(range(pieces))
            for copy in copies + emitted:
                copy.wait()

    pl.run_scoped(
        rear,
        pltpu.VMEM((tokens, tokens), F32),
        pltpu.VMEM((2, tokens, LANES), BF),
        pltpu.VMEM((2, tokens, LANES), BF),
        pltpu.VMEM((2, tokens, LANES), F32),
        pltpu.VMEM((2, tokens, LANES), F32),
        pltpu.VMEM((nd // 2, shard, hidden), BF),
    )


def layer(nt, nd, x, cot, gain_a, gain_f, segr, wq, wkt, wvt, wo, gate, up, down):
    width = nd.bit_length() - 1
    rows, model = x.shape
    tokens = nt * rows
    queries = wq.shape[1]
    hidden = gate.shape[1]
    shard = model // nd
    half = nd // 2
    wide = queries + LANES
    span = max(width_ for _, width_ in tiles_of(hidden, 6))
    shape = jax.ShapeDtypeStruct
    outs = [
        (shape((rows, model), BF), hbm()),
        (shape((rows, model), F32), hbm()),
        (shape((8, shard), F32), hbm()),
        (shape((shard, queries), F32), hbm()),
        (shape((LANES, shard), F32), hbm()),
        (shape((queries, shard), F32), hbm()),
        (shape((hidden, shard), F32), hbm()),
        (shape((shard, hidden), F32), hbm()),
        (shape((shard, hidden), F32), hbm()),
        (shape((model, wide), BF), hbm()),
        (shape((queries, model), BF), hbm()),
        (shape((tokens, model), BF), hbm()),
    ]
    return pl.pallas_call(
        functools.partial(layer_kernel, nt, width),
        out_shape=[o for o, _ in outs],
        in_specs=[vmem()] * 8 + [hbm()] * 4,
        out_specs=[s for _, s in outs],
        scratch_shapes=[
            pltpu.VMEM((tokens, model), BF),
            pltpu.VMEM((tokens, model), BF),
            pltpu.VMEM((tokens, model), BF),
            pltpu.VMEM((tokens, hidden), BF),
            pltpu.VMEM((rows, model), F32),
            pltpu.VMEM((model, hidden), BF),
            pltpu.VMEM((model, hidden), BF),
            pltpu.VMEM((hidden, model), BF),
            pltpu.VMEM((max(tokens, 2 * shard), max(model, 3 * span)), F32),
        ]
        + line_scratch(nt, rows, model)
        + [
            pltpu.VMEM((2, half, shard, hidden), BF),
            pltpu.VMEM((2, 2, half - 1, shard // 2, hidden), BF),
            pltpu.VMEM((shard, hidden), F32),
            pltpu.VMEM((rows, model), BF),
            pltpu.VMEM((rows, model), F32),
            pltpu.VMEM((8, shard), F32),
            pltpu.VMEM((shard, queries), F32),
            pltpu.VMEM((LANES, shard), F32),
            pltpu.VMEM((queries, shard), F32),
            pltpu.VMEM((hidden, shard), F32),
            pltpu.VMEM((shard, wide), BF),
            pltpu.VMEM((8, shard), F32),
            pltpu.VMEM((nd, 8, shard), F32),
            pltpu.VMEM((tokens, queries), BF),
            pltpu.VMEM((tokens, LANES), BF),
            pltpu.VMEM((tokens, queries), BF),
            pltpu.VMEM((tokens, LANES), F32),
            pltpu.VMEM((tokens, LANES), F32),
            pltpu.VMEM((tokens, LANES), F32),
            pltpu.VMEM((8, model), F32),
            pltpu.VMEM((nt, 8, model), F32),
            pltpu.VMEM((nd, 8, shard), F32),
            dma(2, nd),
            dma(7),
            dma(3),
            dma(4, nt, PIECES),
            dma(4, nt, PIECES),
            dma(2, 2, nt, PIECES),
            dma(8, 2, half - 1),
            dma(8, 2, half - 1),
            dma(8, half),
            dma(8, half),
            dma(2, nt),
            dma(2, nd),
            dma(2 * PIECES + 5),
            pltpu.SemaphoreType.REGULAR((2,)),
            pltpu.SemaphoreType.REGULAR((2,)),
        ],
        compiler_params=pltpu.CompilerParams(
            collective_id=0, has_side_effects=True, vmem_limit_bytes=VMEM_BYTES
        ),
        name="layer",
    )(x, cot, gain_a, gain_f, segr, wq, wkt, wvt, wo, gate, up, down)


def hand_over_kernel(count, kv, *refs):
    sources, rest = refs[: count + 2], refs[count + 2 :]
    targets, rest = rest[: count + 4], rest[count + 4 :]
    held, (in_sem, out_sem) = rest[: count + 2], rest[count + 2 :]
    ins = [
        pltpu.make_async_copy(src, buf, in_sem.at[i])
        for i, (src, buf) in enumerate(zip(sources, held))
    ]
    for copy in ins:
        copy.start()
    outs = []
    for i in range(count):
        ins[i].wait()
        outs.append(pltpu.make_async_copy(held[i], targets[i], out_sem.at[i]))
        outs[-1].start()
    ins[count].wait()
    for i in range(2):
        outs.append(
            pltpu.make_async_copy(
                held[count].at[pl.ds(i * kv, kv), :], targets[count + i], out_sem.at[count + i]
            )
        )
        outs[-1].start()
    ins[count + 1].wait()
    gains = held[count + 1]
    for i in range(2):
        targets[count + 2 + i][...] = gains[i, :]
    for copy in outs:
        copy.wait()


def hand_over(arrays, d_kv, gains):
    count, kv = len(arrays), d_kv.shape[0] // 2
    shape = jax.ShapeDtypeStruct
    outs = [shape(a.shape, a.dtype) for a in arrays]
    outs += [shape((kv, d_kv.shape[1]), F32)] * 2 + [shape((gains.shape[1],), F32)] * 2
    inputs = (*arrays, d_kv, gains)
    return pl.pallas_call(
        functools.partial(hand_over_kernel, count, kv),
        out_shape=outs,
        in_specs=[hbm()] * len(inputs),
        out_specs=[hbm()] * (count + 2) + [vmem()] * 2,
        scratch_shapes=[pltpu.VMEM(a.shape, a.dtype) for a in inputs]
        + [dma(len(inputs)), dma(count + 2)],
        compiler_params=pltpu.CompilerParams(vmem_limit_bytes=VMEM_BYTES),
        name="hand_over",
    )(*inputs)


def narrow_scatter(value, axis, scatter_dimension, tiled):
    low = value.astype(BF) if value.ndim == 2 else value
    return lax.psum_scatter(low, axis, scatter_dimension=scatter_dimension, tiled=tiled).astype(F32)


def rope_tables(segments, head_dim):
    row_count = segments.shape[0]
    row_index = jnp.arange(row_count, dtype=jnp.int32)
    change = jnp.concatenate(
        [jnp.ones((1,), jnp.int32), (segments[1:] != segments[:-1]).astype(jnp.int32)]
    )
    starts = lax.cummax(jnp.where(change > 0, row_index, jnp.zeros_like(row_index)), axis=0)
    position = (row_index - starts).astype(F32)
    half_dim = head_dim // 2
    frequency = jnp.exp(jnp.arange(half_dim, dtype=F32) * (-math.log(10000.0) / half_dim))
    angles = position[:, None] * frequency[None, :]
    return (jnp.cos(angles)[:, None, :], jnp.sin(angles)[:, None, :])


def rotate(tensor, cosine, sine):
    half_dim = tensor.shape[-1] // 2
    first_half = tensor[..., :half_dim]
    second_half = tensor[..., half_dim:]
    return jnp.concatenate(
        [first_half * cosine - second_half * sine, second_half * cosine + first_half * sine],
        axis=-1,
    )


def unrotate(tensor, cosine, sine):
    half_dim = tensor.shape[-1] // 2
    first_half = tensor[..., :half_dim]
    second_half = tensor[..., half_dim:]
    return jnp.concatenate(
        [first_half * cosine + second_half * sine, second_half * cosine - first_half * sine],
        axis=-1,
    )


def visible(segments):
    row_index = jnp.arange(segments.shape[0], dtype=jnp.int32)
    same_seq = segments[:, None] == segments[None, :]
    return same_seq & (row_index[:, None] >= row_index[None, :])


def normalize(values, gain):
    inverse = lax.rsqrt(jnp.mean(values * values, axis=-1, keepdims=True) + EPSILON)
    unit_rows = values * inverse
    return (unit_rows, inverse, (unit_rows * gain.astype(F32)).astype(BF))


def normalize_back(grad_normed, unit_rows, inverse, gain):
    scaled = grad_normed * gain.astype(F32)
    grad_values = inverse * (
        scaled - unit_rows * jnp.mean(scaled * unit_rows, axis=-1, keepdims=True)
    )
    return (grad_values, jnp.sum(grad_normed * unit_rows, axis=0))


def contract(left, right, left_dim, right_dim):
    return lax.dot_general(
        left, right, (((left_dim,), (right_dim,)), ((), ())), preferred_element_type=F32
    )


def block_scores(query_block, key_heads, allowed_block, score_scale):
    scores = (
        jnp.einsum("rkgd,skd->kgrs", query_block, key_heads, preferred_element_type=F32)
        * score_scale
    )
    return jnp.where(allowed_block[None, None], scores, NEGATIVE)


def attend_forward(query_groups, key_heads, value_heads, allowed, score_scale):
    scores = block_scores(query_groups, key_heads, allowed, score_scale)
    row_max = jnp.max(scores, axis=-1, keepdims=True)
    log_total = row_max + jnp.log(jnp.sum(jnp.exp(scores - row_max), axis=-1, keepdims=True))
    probs_low = jnp.exp(scores - log_total).astype(BF)
    mixed_parts = jnp.einsum(
        "kgrs,skd->rkgd", probs_low, value_heads, preferred_element_type=F32
    ).astype(BF)
    return (mixed_parts, log_total)


def attend_backward(
    query_groups, key_heads, value_heads, mixed_heads, grad_mixed, log_totals, allowed, score_scale
):
    scores = block_scores(query_groups, key_heads, allowed, score_scale)
    attn_probs = jnp.exp(scores - log_totals)
    probs_low = attn_probs.astype(BF)
    grad_probs = jnp.einsum(
        "rkgd,skd->kgrs", grad_mixed, value_heads, preferred_element_type=F32
    )
    row_delta = jnp.sum(grad_mixed.astype(F32) * mixed_heads.astype(F32), axis=-1)
    row_delta = jnp.transpose(row_delta, (1, 2, 0))[..., None]
    grad_scores = (attn_probs * (grad_probs - row_delta)).astype(BF)
    query_parts = (
        jnp.einsum("kgrs,skd->rkgd", grad_scores, key_heads, preferred_element_type=F32)
        * score_scale
    )
    grad_key_rot = (
        jnp.einsum("kgrs,rkgd->skd", grad_scores, query_groups, preferred_element_type=F32)
        * score_scale
    )
    grad_value_heads = jnp.einsum(
        "kgrs,rkgd->skd", probs_low, grad_mixed, preferred_element_type=F32
    )
    return (query_parts, grad_key_rot, grad_value_heads)


def plain_device(
    layer_input,
    segment_ids,
    norm_attn,
    w_query,
    w_key,
    w_value,
    w_output,
    norm_ffn,
    w_gate,
    w_up,
    w_down,
    cotangent,
):
    score_scale = HD ** (-0.5)
    query_full, key_full, value_full, output_full, gain_attn = (
        lax.all_gather(w_query, "dp", axis=0, tiled=True),
        lax.all_gather(w_key, "dp", axis=0, tiled=True),
        lax.all_gather(w_value, "dp", axis=0, tiled=True),
        lax.all_gather(w_output, "dp", axis=1, tiled=True),
        lax.all_gather(norm_attn, "dp", axis=0, tiled=True),
    )
    gate_full, up_full, down_full, gain_ffn = (
        lax.all_gather(w_gate, "dp", axis=0, tiled=True),
        lax.all_gather(w_up, "dp", axis=0, tiled=True),
        lax.all_gather(w_down, "dp", axis=1, tiled=True),
        lax.all_gather(norm_ffn, "dp", axis=0, tiled=True),
    )
    heads_local = query_full.shape[1] // HD
    kv_local = key_full.shape[1] // HD
    group = heads_local // kv_local
    residual_in = layer_input.astype(F32)
    unit_attn, inverse_attn, normed_local = normalize(residual_in, gain_attn)
    normed_attn = lax.all_gather(normed_local, "tensor", axis=0, tiled=True)
    row_count = normed_attn.shape[0]
    cosine, sine = rope_tables(segment_ids, HD)
    allowed = visible(segment_ids)
    query_heads = rotate(
        jnp.dot(normed_attn, query_full, preferred_element_type=F32).reshape(
            row_count, heads_local, HD
        ),
        cosine,
        sine,
    ).astype(BF)
    query_groups = query_heads.reshape(row_count, kv_local, group, HD)
    key_heads = rotate(
        jnp.dot(normed_attn, key_full, preferred_element_type=F32).reshape(
            row_count, kv_local, HD
        ),
        cosine,
        sine,
    ).astype(BF)
    value_heads = (
        jnp.dot(normed_attn, value_full, preferred_element_type=F32)
        .astype(BF)
        .reshape(row_count, kv_local, HD)
    )
    mixed_heads, log_totals = attend_forward(
        query_groups, key_heads, value_heads, allowed, score_scale
    )
    mixed_flat = mixed_heads.reshape(row_count, heads_local * HD)
    hidden_res = residual_in + narrow_scatter(
        jnp.dot(mixed_flat, output_full, preferred_element_type=F32),
        "tensor",
        scatter_dimension=0,
        tiled=True,
    )
    unit_ffn, inverse_ffn, normed_ffn_local = normalize(hidden_res, gain_ffn)
    normed_ffn = lax.all_gather(normed_ffn_local, "tensor", axis=0, tiled=True)
    gate_rows = jnp.dot(normed_ffn, gate_full, preferred_element_type=F32)
    up_rows = jnp.dot(normed_ffn, up_full, preferred_element_type=F32)
    sigmoid_gate = jax.nn.sigmoid(gate_rows)
    active = (gate_rows * sigmoid_gate * up_rows).astype(BF)
    layer_output = (
        hidden_res
        + narrow_scatter(
            jnp.dot(active, down_full, preferred_element_type=F32).astype(BF),
            "tensor",
            scatter_dimension=0,
            tiled=True,
        ).astype(F32)
    ).astype(BF)
    query_full, key_full, value_full, output_full, gate_full, up_full, down_full = (
        lax.all_gather(w_query, "dp", axis=0, tiled=True),
        lax.all_gather(w_key, "dp", axis=0, tiled=True),
        lax.all_gather(w_value, "dp", axis=0, tiled=True),
        lax.all_gather(w_output, "dp", axis=1, tiled=True),
        lax.all_gather(w_gate, "dp", axis=0, tiled=True),
        lax.all_gather(w_up, "dp", axis=0, tiled=True),
        lax.all_gather(w_down, "dp", axis=1, tiled=True),
    )
    cotangent_full = lax.all_gather(cotangent, "tensor", axis=0, tiled=True)
    grad_active = contract(cotangent_full, down_full, 1, 1)
    grad_w_down = contract(active, cotangent_full, 0, 0)
    grad_up_rows = (grad_active * gate_rows * sigmoid_gate).astype(BF)
    grad_gate_rows = (
        grad_active * up_rows * sigmoid_gate * (1.0 + gate_rows * (1.0 - sigmoid_gate))
    ).astype(BF)
    grad_w_gate = contract(normed_ffn, grad_gate_rows, 0, 0)
    grad_w_up = contract(normed_ffn, grad_up_rows, 0, 0)
    grad_normed_ffn = narrow_scatter(
        contract(grad_gate_rows, gate_full, 1, 1) + contract(grad_up_rows, up_full, 1, 1),
        "tensor",
        scatter_dimension=0,
        tiled=True,
    )
    grad_hidden, gain_ffn_part = normalize_back(grad_normed_ffn, unit_ffn, inverse_ffn, gain_ffn)
    grad_hidden = cotangent.astype(F32) + grad_hidden
    branch_full = lax.all_gather(grad_hidden.astype(BF), "tensor", axis=0, tiled=True)
    grad_mixed = contract(branch_full, output_full, 1, 1).astype(BF)
    grad_w_output = contract(mixed_flat, branch_full, 0, 0)
    grad_query_rot, grad_key_rot, grad_value_heads = attend_backward(
        query_groups,
        key_heads,
        value_heads,
        mixed_heads,
        grad_mixed.reshape(row_count, kv_local, group, HD),
        log_totals,
        allowed,
        score_scale,
    )
    grad_queries = (
        unrotate(grad_query_rot.reshape(row_count, heads_local, HD), cosine, sine)
        .reshape(row_count, heads_local * HD)
        .astype(BF)
    )
    grad_keys = (
        unrotate(grad_key_rot, cosine, sine).reshape(row_count, kv_local * HD).astype(BF)
    )
    grad_values = grad_value_heads.reshape(row_count, kv_local * HD).astype(BF)
    grad_w_query = contract(normed_attn, grad_queries, 0, 0)
    grad_w_key = contract(normed_attn, grad_keys, 0, 0)
    grad_w_value = contract(normed_attn, grad_values, 0, 0)
    grad_normed_attn = narrow_scatter(
        contract(grad_queries, query_full, 1, 1)
        + contract(grad_keys, key_full, 1, 1)
        + contract(grad_values, value_full, 1, 1),
        "tensor",
        scatter_dimension=0,
        tiled=True,
    )
    grad_residual, gain_attn_part = normalize_back(
        grad_normed_attn, unit_attn, inverse_attn, gain_attn
    )
    grad_input = grad_hidden + grad_residual
    gain_attn_total, gain_ffn_total = lax.psum((gain_attn_part, gain_ffn_part), "tensor")
    owned = (
        narrow_scatter(grad_w_query, "dp", scatter_dimension=0, tiled=True),
        narrow_scatter(grad_w_key, "dp", scatter_dimension=0, tiled=True),
        narrow_scatter(grad_w_value, "dp", scatter_dimension=0, tiled=True),
        narrow_scatter(grad_w_output, "dp", scatter_dimension=1, tiled=True),
        narrow_scatter(gain_attn_total, "dp", scatter_dimension=0, tiled=True),
        narrow_scatter(gain_ffn_total, "dp", scatter_dimension=0, tiled=True),
        narrow_scatter(grad_w_gate, "dp", scatter_dimension=0, tiled=True),
        narrow_scatter(grad_w_up, "dp", scatter_dimension=0, tiled=True),
        narrow_scatter(grad_w_down, "dp", scatter_dimension=1, tiled=True),
    )
    return (
        layer_output,
        grad_input,
        owned[4],
        owned[0],
        owned[1],
        owned[2],
        owned[3],
        owned[5],
        owned[6],
        owned[7],
        owned[8],
    )


def with_kernels(nt, nd, layer_input, segment_ids, norm_attn, w_query, w_key, w_value, w_output, norm_ffn, w_gate, w_up, w_down, cotangent):
    y, gi, gains, d_wq, d_kv, d_wo, d_down, d_gate, d_up, *_ = layer(
        nt, nd, layer_input, cotangent, norm_attn, norm_ffn, segment_ids[None, :],
        w_query, w_key.T, w_value.T, w_output, w_gate, w_up, w_down,
    )
    y, gi, d_wq, d_wo, d_gate, d_up, d_down, d_k, d_v, d_attn, d_ffn = hand_over(
        (y, gi, d_wq, d_wo, d_gate, d_up, d_down), d_kv, gains
    )
    return (y, gi, d_attn, d_wq, d_k.T, d_v.T, d_wo, d_ffn, d_gate, d_up, d_down)


def fits(nt, nd, shards):
    layer_input, segment_ids, norm_attn, w_query, w_key, w_value, w_output, norm_ffn, w_gate, w_up, w_down, _ = shards
    return (
        nd >= 4
        and nd & (nd - 1) == 0
        and nt >= 2
        and norm_attn.shape[0] % LANES == 0
        and w_output.shape[1] % LANES == 0
        and w_gate.shape[1] % LANES == 0
        and w_query.shape[1] % LANES == 0
        and w_key.shape[1] == HD
        and segment_ids.shape[0] == nt * layer_input.shape[0]
        and segment_ids.shape[0] % LANES == 0
    )


def on_device(nt, nd, *shards):
    if fits(nt, nd, shards):
        return with_kernels(nt, nd, *shards)
    return plain_device(*shards)


def solution(mesh):
    placed = (
        P(("dp", "tensor"), None),
        P("dp"),
        P("dp"),
        P("dp", "tensor"),
        P("dp", "tensor"),
        P("dp", "tensor"),
        P("tensor", "dp"),
        P("dp"),
        P("dp", "tensor"),
        P("dp", "tensor"),
        P("tensor", "dp"),
        P(("dp", "tensor"), None),
    )
    return jax.shard_map(
        functools.partial(on_device, mesh.shape["tensor"], mesh.shape["dp"]),
        mesh=mesh,
        in_specs=placed,
        out_specs=(
            P(("dp", "tensor"), None),
            P(("dp", "tensor"), None),
            P("dp"),
            P("dp", "tensor"),
            P("dp", "tensor"),
            P("dp", "tensor"),
            P("tensor", "dp"),
            P("dp"),
            P("dp", "tensor"),
            P("dp", "tensor"),
            P("tensor", "dp"),
        ),
        check_vma=False,
    )
```

profile of v0, /device:TPU:0, one launch (start us, length us, event | category | flops | bytes accessed | tf_op | source)
XLA Modules:
  0.0 269.8 jit_solution(2734279748778854411)
XLA Ops:
  0.6 262.7 %layer.1 = (bf16[128,2048]{1,0:T(8,128)(2,1)}, f32[128,2048]{1,0:T(8,128)}, f32[8,256]{1,0:T(8,128)}, f32[256,512]{1,0:T(8,128)}, f32[128,256]{1,0:T(8,128)}, /*...) custom-call(bf16[128,2048]{1,0:T(8,128)(2,1)} %x.1, ...), custom_call_target="tpu_custom_call" | custom-call | tf_op jit(solution)/shard_map/layer/pallas_call | solution.py:1376
  263.3 6.4 %hand_over.1 = (bf16[128,2048]{1,0:T(8,128)(2,1)}, f32[128,2048]{1,0:T(8,128)}, f32[256,512]{1,0:T(8,128)}, f32[512,256]{1,0:T(8,128)}, f32[256,1408]{1,0:T(8,12...) custom-call(bf16[128,2048]{1,0:T(8,128)(2,1)} %get-tuple-element.31., ...), custom_call_target="tpu_custom_call" | custom-call | tf_op jit(solution)/shard_map/hand_over/pallas_call | solution.py:1476
where the time goes:
time: 270 us
  Pallas kernels  269 us (100%)
    pallas_call x1, Pallas kernels, layer(): pl.pallas_call(functools.partial(layer_kernel, nt, width), out_shape=[o f...  263 us
    pallas_call x1, Pallas kernels, hand_over(): pl.pallas_call(functools.partial(hand_over_kernel, count, kv), out_shape=...  6.35 us

commit v1 on v0

--- a/solution.py
+++ b/solution.py
@@ -206,7 +206,7 @@
         return pl.ds(aligned(self.row(j, s), self.size), self.size)
 
     def mine(self, j, s):
-        return self.part[self.rows(j, s), : self.model]
+        return self.part[self.rows(j, s), : self.model].astype(F32)
 
     def edge(self, s):
         t, nt = self.t, self.nt
@@ -244,6 +244,14 @@
                 self.part[rows, : self.model] += self.arrived[self.slot(way, t), self.sub(s), :].astype(F32)
 
         return rows
+
+    def own_into(self, s, total, at):
+        total[at, :] += self.mine(self.t, s)
+        for way in (self.near, self.far):
+            @pl.when(self.depth(way) > 0)
+            def _():
+                self.move(way, self.t, s).wait_recv()
+                total[at, :] += self.arrived[self.slot(way, self.t), self.sub(s), :].astype(F32)
 
     def finish(self, pieces):
         for way in range(2):
@@ -580,10 +588,10 @@
     nt, width,
     x, cot, gain_a, gain_f, segr, wq, wkt, wvt, wo, gate, up, down,
     y_o, gi_o, gain_o, d_wq_o, d_kv_o, d_wo_o, d_down_o, d_gate, d_up, wqkv_f, wo_f, na_f,
-    rowsbuf, cf, branch, act, hid, gate_v, up_v, down_v, part, sent, arrived, totals, landed, stage_v,
-    y, gi, gain_out, d_wq, d_kv, d_wo, d_down,
+    rowsbuf, cf, branch, act, hid, gate_v, up_v, down_v, part, sent, arrived, y_arrived, totals, landed, stage_v,
+    y, gi, gain_out, d_kv, d_down,
     own_qkv, gain, gall, qo, kvo, mo, lo, cos, sin, gsum, zslots, dslots,
-    gain_sem, place_sem, out_sem, line_sem, cot_sem, sum_sem,
+    gain_sem, place_sem, out_sem, line_sem, cot_sem, sum_sem, first_sem,
     hs, hr, ps, pr, zsem, dsem, emit_sem, ready, calm,
 ):
     me, t = lax.axis_index("dp"), lax.axis_index("tensor")
@@ -802,11 +810,11 @@
         d_down[:, at] = value.T
 
     def store_qkv(at, value):
-        d_wq[at, :] = value[:, :queries]
+        stage_v[at, :queries] = value[:, :queries]
         d_kv[:, at] = value[:, queries:].T
 
     def store_wo(at, value):
-        d_wo[:, at] = value.T
+        part[:queries, model + at.start : model + at.stop] = value.T
 
     for_qkv, for_wo = pl.ds(0, wide), pl.ds(wide, queries)
     s_gate = cube(5, totals.at[0], landed.at[0], store_stage)
@@ -863,488 +871,521 @@
     gsum[...] = jnp.zeros_like(gsum)
     gather_br = LineGather(branch, natural, size, t, nt, line_sem)
 
-    def feed(dg, du, given):
-        cuts = tiles_of(hidden, 6)
-        span = max(width_ for _, width_ in cuts)
-        half = tokens // 2
-        block = 64
-
-        def tile_in(h, i):
-            start, width_ = cuts[i]
-            at = slice(start, start + width_)
-            held = mine = slice(h * half, (h + 1) * half)
-            part[held, 0:width_] = dot(rowsbuf[mine, :], gate_v[:, at])
-            part[held, span : span + width_] = dot(rowsbuf[mine, :], up_v[:, at])
-
-        def tile_out(h, i):
-            start, width_ = cuts[i]
-            at = slice(start, start + width_)
-            held = mine = slice(h * half, (h + 1) * half)
-            part[held, 2 * span : 2 * span + width_] = dot(cf[mine, :], down_v[at, :], 1, 1)
-
-            @pl.loop(0, half // block)
-            def _(k):
-                from_ = pl.ds(pl.multiple_of(h * half + k * block, block), block)
-                to = pl.ds(pl.multiple_of(h * half + k * block, block), block)
-                g = part[from_, 0:width_]
-                u = part[from_, span : span + width_]
-                ga = part[from_, 2 * span : 2 * span + width_]
-                sig = 1.0 / (1.0 + jnp.exp(-g))
-                gs = g * sig
-                act[to, at] = (gs * u).astype(BF)
-                du[to, at] = (ga * gs).astype(BF)
-                dg[to, at] = (ga * u * sig * (1.0 + g * (1.0 - sig))).astype(BF)
-
-        def tile(h, i):
+    def second_part(y_first, y_sent):
+        scatter_ya = LineScatter(y_first, shuffled, y_sent, y_arrived, t, nt, first_sem)
+
+        def feed(dg, du, given):
+            cuts = tiles_of(hidden, 6)
+            span = max(width_ for _, width_ in cuts)
+            half = tokens // 2
+            block = 64
+
+            def tile_in(h, i):
+                start, width_ = cuts[i]
+                at = slice(start, start + width_)
+                held = mine = slice(h * half, (h + 1) * half)
+                part[held, 0:width_] = dot(rowsbuf[mine, :], gate_v[:, at])
+                part[held, span : span + width_] = dot(rowsbuf[mine, :], up_v[:, at])
+
+            def tile_out(h, i):
+                start, width_ = cuts[i]
+                at = slice(start, start + width_)
+                held = mine = slice(h * half, (h + 1) * half)
+                part[held, 2 * span : 2 * span + width_] = dot(cf[mine, :], down_v[at, :], 1, 1)
+
+                @pl.loop(0, half // block)
+                def _(k):
+                    from_ = pl.ds(pl.multiple_of(h * half + k * block, block), block)
+                    to = pl.ds(pl.multiple_of(h * half + k * block, block), block)
+                    g = part[from_, 0:width_]
+                    u = part[from_, span : span + width_]
+                    ga = part[from_, 2 * span : 2 * span + width_]
+                    sig = 1.0 / (1.0 + jnp.exp(-g))
+                    gs = g * sig
+                    act[to, at] = (gs * u).astype(BF)
+                    du[to, at] = (ga * gs).astype(BF)
+                    dg[to, at] = (ga * u * sig * (1.0 + g * (1.0 - sig))).astype(BF)
+
+            def tile(h, i):
+                with scope("tile"):
+                    tile_in(h, i)
+                    tile_out(h, i)
+
+            def back_dots(h):
+                mine = slice(h * half, (h + 1) * half)
+
+                def product(cols):
+                    part[mine, cols] = dot(dg[mine, :], gate_v[cols, :], 1, 1) + dot(
+                        du[mine, :], up_v[cols, :], 1, 1
+                    )
+
+                over_cols(model, cut, product)
+
+            scatter_gn = LineScatter(part, shuffled, sent, arrived, t, nt, sum_sem)
+
+            def take_grad(s):
+                at = scatter_gn.own(s)
+                block_ = slice(s * size, (s + 1) * size)
+                there = pl.ds(pl.multiple_of(natural(t, s), size), size)
+
+                def store(cols, value):
+                    total = cot[block_, cols].astype(F32) + value
+                    gi[block_, cols] = total
+                    branch[there, cols] = total.astype(BF)
+
+                def store_gain(cols, value):
+                    gsum[1:2, cols] += value
+
+                back_through_norm(
+                    lambda c: hid[block_, c], lambda c: part[at, c], gall, 1, store, store_gain
+                )
+                gather_br.start(s)
+
+            s_gate.chunk, s_up.chunk = chunk_of(rowsbuf, dg), chunk_of(rowsbuf, du)
+            s_gate.sent = s_up.sent = given
+
+            half_a, half_b = range(first_half), range(first_half, pieces)
+            def o_near(s):
+                with scope("o_near"):
+                    scatter_o.relay(scatter_o.near, s)
+
+            def o_far(s):
+                with scope("o_far"):
+                    scatter_o.relay(scatter_o.far, s)
+
+            def o_take(s):
+                with scope("o_take"):
+                    take_hidden(s)
+
+            def nf(k, s):
+                with scope("nf_step"):
+                    gather_nf.step(k, s)
+
+            def cot_steps(k, which):
+                with scope("cot_step"):
+                    for s in which:
+                        cots.step(k, s)
+
+            def gn_near(s):
+                with scope("gn_near"):
+                    scatter_gn.relay(scatter_gn.near, s)
+
+            def gn_far(s):
+                with scope("gn_far"):
+                    scatter_gn.relay(scatter_gn.far, s)
+
+            def ya_near(s):
+                with scope("ya_near"):
+                    scatter_ya.relay(scatter_ya.near, s)
+
+            def ya_far(s):
+                with scope("ya_far"):
+                    scatter_ya.relay(scatter_ya.far, s)
+
+            def gn_take(s):
+                with scope("gn_take"):
+                    take_grad(s)
+
+            def weight(g, stage):
+                with scope("weight"):
+                    if stage < stages:
+                        forward(g, stage)
+
+            scatter_o.edge(0)
+            scatter_o.edge(1)
+            cot_steps(1, half_a)
+            weight(g_gate, 1)
+            cot_steps(2, half_a)
+            o_near(0)
+            weight(g_up, 0)
+            o_far(0)
+            o_take(0)
+            weight(g_down, 0)
+            scatter_o.edge(2)
+            o_near(1)
+            o_far(1)
+            nf(1, 0)
+            cot_steps(3, half_a)
+            o_take(1)
+            scatter_o.edge(3)
+            nf(1, 1)
+            nf(2, 0)
+            o_near(2)
+            nf(2, 1)
+            weight(g_up, 1)
+            o_far(2)
+            o_near(3)
+            nf(3, 0)
+            for s in half_b:
+                cots.start(s)
+            nf(3, 1)
+            o_take(2)
+            o_far(3)
+            gather_nf.complete(half_a)
+            cots.complete(half_a)
+            weight(g_down, 1)
+            for stage in range(2, stages):
+                for g in (g_gate, g_up, g_down):
+                    weight(g, stage)
+            with scope("wait_ffn"):
+                for w in (2, 3):
+                    gathers[w].place(place_sem.at[w]).wait()
+                    gathers[w].pair_wait()
             with scope("tile"):
-                tile_in(h, i)
-                tile_out(h, i)
-
-        def back_dots(h):
-            mine = slice(h * half, (h + 1) * half)
-
-            def product(cols):
-                part[mine, cols] = dot(dg[mine, :], gate_v[cols, :], 1, 1) + dot(
-                    du[mine, :], up_v[cols, :], 1, 1
-                )
-
-            over_cols(model, cut, product)
-
-        scatter_gn = LineScatter(part, shuffled, sent, arrived, t, nt, sum_sem)
-
-        def take_grad(s):
-            at = scatter_gn.own(s)
-            block_ = slice(s * size, (s + 1) * size)
-            there = pl.ds(pl.multiple_of(natural(t, s), size), size)
-
-            def store(cols, value):
-                total = cot[block_, cols].astype(F32) + value
-                gi[block_, cols] = total
-                branch[there, cols] = total.astype(BF)
-
-            def store_gain(cols, value):
-                gsum[1:2, cols] += value
-
-            back_through_norm(
-                lambda c: hid[block_, c], lambda c: part[at, c], gall, 1, store, store_gain
-            )
-            gather_br.start(s)
-
-        s_gate.chunk, s_up.chunk = chunk_of(rowsbuf, dg), chunk_of(rowsbuf, du)
-        s_gate.sent = s_up.sent = given
-
-        half_a, half_b = range(first_half), range(first_half, pieces)
-        def o_near(s):
-            with scope("o_near"):
-                scatter_o.relay(scatter_o.near, s)
-
-        def o_far(s):
-            with scope("o_far"):
-                scatter_o.relay(scatter_o.far, s)
-
-        def o_take(s):
-            with scope("o_take"):
-                take_hidden(s)
-
-        def nf(k, s):
-            with scope("nf_step"):
-                gather_nf.step(k, s)
-
-        def cot_steps(k, which):
-            with scope("cot_step"):
-                for s in which:
-                    cots.step(k, s)
-
-        def gn_near(s):
-            with scope("gn_near"):
-                scatter_gn.relay(scatter_gn.near, s)
-
-        def gn_far(s):
-            with scope("gn_far"):
-                scatter_gn.relay(scatter_gn.far, s)
-
-        def gn_take(s):
-            with scope("gn_take"):
-                take_grad(s)
-
-        def weight(g, stage):
-            with scope("weight"):
-                if stage < stages:
-                    forward(g, stage)
-
-        scatter_o.edge(0)
-        scatter_o.edge(1)
-        cot_steps(1, half_a)
-        weight(g_gate, 1)
-        cot_steps(2, half_a)
-        o_near(0)
-        weight(g_up, 0)
-        o_far(0)
-        o_take(0)
-        weight(g_down, 0)
-        scatter_o.edge(2)
-        o_near(1)
-        o_far(1)
-        nf(1, 0)
-        cot_steps(3, half_a)
-        o_take(1)
-        scatter_o.edge(3)
-        nf(1, 1)
-        nf(2, 0)
-        o_near(2)
-        nf(2, 1)
-        weight(g_up, 1)
-        nf(3, 0)
-        o_far(2)
-        for s in half_b:
-            cots.start(s)
-        nf(3, 1)
-        o_take(2)
-        gather_nf.complete(half_a)
-        cots.complete(half_a)
-        weight(g_down, 1)
-        for stage in range(2, stages):
-            for g in (g_gate, g_up, g_down):
-                weight(g, stage)
-        o_near(3)
-        with scope("wait_ffn"):
-            for w in (2, 3):
-                gathers[w].place(place_sem.at[w]).wait()
-                gathers[w].pair_wait()
-        with scope("tile"):
-            tile_in(0, 0)
-        with scope("wait_ffn"):
-            g_down.place(place_sem.at[4]).wait()
-            g_down.pair_wait()
-        with scope("tile"):
-            tile_out(0, 0)
-        o_far(3)
-        nf(1, 2)
-        cot_steps(1, half_b)
-        for i in range(1, len(cuts)):
-            tile(0, i)
-        o_take(3)
-        nf(2, 2)
-        with scope("back_dots"):
-            scatter_o.finish(half_a)
-            back_dots(0)
-        scatter_gn.edge(0)
-        scatter_gn.edge(1)
-        nf(1, 3)
-        cot_steps(2, half_b)
-        gn_near(0)
-        nf(3, 2)
-        nf(2, 3)
-        gn_far(0)
-        cot_steps(3, half_b)
-        gn_near(1)
-        nf(3, 3)
-        gather_nf.complete(half_b)
-        cots.complete(half_b)
-        gather_nf.finish(half_a)
-        tile(1, 0)
-        gn_far(1)
-        gn_take(0)
-        for i in range(1, len(cuts)):
-            tile(1, i)
-        with scope("back_dots"):
-            scatter_o.finish(half_b)
-            back_dots(1)
-        scatter_gn.edge(2)
-        gn_take(1)
-        scatter_gn.edge(3)
-        br(1, 0)
-        with scope("gn_fill"):
-            s_gate.give()
+                tile_in(0, 0)
+            with scope("wait_ffn"):
+                g_down.place(place_sem.at[4]).wait()
+                g_down.pair_wait()
+            with scope("tile"):
+                tile_out(0, 0)
+            o_take(3)
+            nf(1, 2)
+            cot_steps(1, half_b)
+            for i in range(1, len(cuts)):
+                tile(0, i)
+            nf(2, 2)
+            nf(1, 3)
+            with scope("back_dots"):
+                scatter_o.finish(half_a)
+                back_dots(0)
+            scatter_gn.edge(0)
+            scatter_gn.edge(1)
+            cot_steps(2, half_b)
+            with scope("y_part"):
+                def product(cols):
+                    y_first[:, cols] = dot(act[: tokens // 2, :], down_v[:, cols]).astype(BF)
+
+                over_cols(model, cut, product)
+            gn_near(0)
+            scatter_ya.edge(0)
+            nf(3, 2)
+            nf(2, 3)
+            gn_far(0)
+            cot_steps(3, half_b)
+            gn_near(1)
+            nf(3, 3)
+            gather_nf.complete(half_b)
+            cots.complete(half_b)
+            gather_nf.finish(half_a)
+            tile(1, 0)
+            gn_far(1)
+            gn_take(0)
+            for i in range(1, len(cuts)):
+                tile(1, i)
+            with scope("back_dots"):
+                scatter_o.finish(half_b)
+                back_dots(1)
+            scatter_gn.edge(2)
+            gn_take(1)
+            scatter_gn.edge(3)
+            with scope("gn_fill"):
+                s_gate.give()
+            br(1, 0)
+            with scope("gn_fill"):
+                take(s_gate)
+            gn_near(2)
             br(2, 0)
-            take(s_gate)
-        gn_near(2)
-        with scope("gn_fill"):
-            s_gate.given()
-            s_up.give()
-        gn_far(2)
-        br(1, 1)
-        br(3, 0)
-        with scope("gn_fill"):
-            take(s_up)
-        gn_near(3)
-        gather_nf.finish(half_b)
-        gn_take(2)
-        y_part(0)
-        scatter_gn.finish(half_a)
-        scatter_y.edge(0)
-        br(2, 1)
-        gn_far(3)
-        gn_take(3)
-        scatter_y.edge(1)
-        br(3, 1)
-        br(1, 2)
-        y_near(0)
-        y_part(1)
-        br(2, 2)
-        br(1, 3)
-        scatter_gn.finish(half_b)
-        scatter_y.edge(2)
-        scatter_y.edge(3)
-        y_far(0)
-        br(3, 2)
-        br(2, 3)
-        with scope("add0"):
-            on(s_gate, 0)
-        y_near(1)
-        y_far(1)
-        br(3, 3)
-        gather_br.complete(range(pieces))
-        s_up.given()
-
-    pl.run_scoped(
-        feed,
-        pltpu.VMEM((tokens, hidden), BF),
-        pltpu.VMEM((tokens, hidden), BF),
-        pltpu.VMEM((nd // 2, shard, hidden), BF),
-    )
-
-    wo_v = down_v.at[pl.ds(0, queries), :]
-    na_v = down_v.at[pl.ds(queries, tokens), :]
-    wqkv_v = gate_v.at[:, pl.ds(0, wide)]
-    gm = up_v.at[pl.ds(0, tokens), pl.ds(0, queries)]
-    dqkv = up_v.at[pl.ds(tokens, tokens), pl.ds(0, wide)]
-
-    def rear(bias, kpad, vpad, dkey, dval, given):
-        inward = LineScatter(part, shuffled, sent, arrived, t, nt, sum_sem)
-        for g in gathers:
-            g.drain()
-        loads = [
-            pltpu.make_async_copy(wo_f, wo_v, place_sem.at[0]),
-            pltpu.make_async_copy(wqkv_f, wqkv_v, place_sem.at[1]),
-            pltpu.make_async_copy(na_f, na_v, place_sem.at[2]),
-        ]
-        for load in loads:
-            load.start()
-        bias_into(bias, segr)
-        pad_pair(kvo[...].astype(F32), kpad, vpad)
-        dkey[...] = jnp.zeros_like(dkey)
-        dval[...] = jnp.zeros_like(dval)
-        s_down.chunk, s_down.sent = chunk_of(cf, act), given
-        s_qkv.chunk, s_qkv.sent = chunk_of(na_v, dqkv), given.at[:, :, for_qkv]
-        s_out.chunk, s_out.sent = chunk_of(branch, mo), given.at[:, :, for_wo]
-
-        def att(first, last):
-            with scope("b_att"):
-                attend_back_pairs(
-                    first, last, qo, gm, mo, lo, kpad, vpad, bias, cos, sin, dqkv, dkey, dval
-                )
-
-        def free(s, out, slot):
-            s.add(stages - 1)
-            copy = pltpu.make_async_copy(stage_v, out, out_sem.at[1 + slot])
-            copy.start()
-            s.drain()
-            for bit in range(width):
-                pl.semaphore_signal(
-                    ready.at[slot], inc=1, device_id={"dp": flip(me, 1 << bit, width)},
-                    device_id_type=pl.DeviceIdType.MESH,
-                )
-            return copy
-
-        def quiet(h):
-            for step, there in ((-1, t > 0), (1, t < nt - 1)):
-                @pl.when(there)
-                def _():
+            with scope("gn_fill"):
+                s_gate.given()
+                s_up.give()
+            gn_far(2)
+            br(1, 1)
+            br(3, 0)
+            with scope("gn_fill"):
+                take(s_up)
+            gn_near(3)
+            gather_nf.finish(half_b)
+            gn_take(2)
+            scatter_ya.edge(1)
+            gn_far(3)
+            ya_near(0)
+            gn_take(3)
+            with scope("add0"):
+                on(s_gate, 0)
+            br(2, 1)
+            br(1, 2)
+            br(3, 1)
+            ya_far(0)
+            y_part(1)
+            br(2, 2)
+            br(1, 3)
+            scatter_gn.finish(half_b)
+            scatter_y.edge(2)
+            scatter_y.edge(3)
+            br(3, 2)
+            br(2, 3)
+            ya_near(1)
+            with scope("add0"):
+                on(s_up, 0)
+            scatter_gn.finish(half_a)
+            s_up.given()
+
+        pl.run_scoped(
+            feed,
+            pltpu.VMEM((tokens, hidden), BF),
+            pltpu.VMEM((tokens, hidden), BF),
+            pltpu.VMEM((nd // 2, shard, hidden), BF),
+        )
+
+        wo_v = down_v.at[pl.ds(0, queries), :]
+        na_v = down_v.at[pl.ds(queries, tokens), :]
+        wqkv_v = gate_v.at[:, pl.ds(0, wide)]
+        gm = up_v.at[pl.ds(0, tokens), pl.ds(0, queries)]
+        dqkv = up_v.at[pl.ds(tokens, tokens), pl.ds(0, wide)]
+
+        def rear(bias, kpad, vpad, dkey, dval, given):
+            inward = LineScatter(part, shuffled, sent, arrived, t, nt, sum_sem)
+            for g in gathers:
+                g.drain()
+            loads = [
+                pltpu.make_async_copy(wo_f, wo_v, place_sem.at[0]),
+                pltpu.make_async_copy(wqkv_f, wqkv_v, place_sem.at[1]),
+                pltpu.make_async_copy(na_f, na_v, place_sem.at[2]),
+            ]
+            for load in loads:
+                load.start()
+            bias_into(bias, segr)
+            pad_pair(kvo[...].astype(F32), kpad, vpad)
+            dkey[...] = jnp.zeros_like(dkey)
+            dval[...] = jnp.zeros_like(dval)
+            s_down.chunk, s_down.sent = chunk_of(cf, act), given
+            s_qkv.chunk, s_qkv.sent = chunk_of(na_v, dqkv), given.at[:, :, for_qkv]
+            s_out.chunk, s_out.sent = chunk_of(branch, mo), given.at[:, :, for_wo]
+
+            def att(first, last):
+                with scope("b_att"):
+                    attend_back_pairs(
+                        first, last, qo, gm, mo, lo, kpad, vpad, bias, cos, sin, dqkv, dkey, dval
+                    )
+
+            def freed(out, slot):
+                return pltpu.make_async_copy(stage_v, out, out_sem.at[1 + slot])
+
+            def free(s, out, slot):
+                s.add(stages - 1)
+                freed(out, slot).start()
+                s.drain()
+                for bit in range(width):
                     pl.semaphore_signal(
-                        calm.at[h], inc=1, device_id={"tensor": t + step},
+                        ready.at[slot], inc=1, device_id={"dp": flip(me, 1 << bit, width)},
                         device_id_type=pl.DeviceIdType.MESH,
                     )
 
-        def gi_part(h):
-            which = half_a if h == 0 else half_b
-            mine = jnp.concatenate(
-                [dqkv[natural(j, s) : natural(j, s) + size, :] for s in which for j in range(nt)],
-                axis=0,
-            )
-            start_row = h * (tokens // 2)
-            with scope("b_part"):
-
-                def product(cols):
-                    part[start_row : start_row + tokens // 2, cols] = dot(
-                        mine, wqkv_v[cols, :], 1, 1
+            def quiet(h):
+                for step, there in ((-1, t > 0), (1, t < nt - 1)):
+                    @pl.when(there)
+                    def _():
+                        pl.semaphore_signal(
+                            calm.at[h], inc=1, device_id={"tensor": t + step},
+                            device_id_type=pl.DeviceIdType.MESH,
+                        )
+
+            def gi_part(h):
+                which = half_a if h == 0 else half_b
+                mine = jnp.concatenate(
+                    [dqkv[natural(j, s) : natural(j, s) + size, :] for s in which for j in range(nt)],
+                    axis=0,
+                )
+                start_row = h * (tokens // 2)
+                with scope("b_part"):
+
+                    def product(cols):
+                        part[start_row : start_row + tokens // 2, cols] = dot(
+                            mine, wqkv_v[cols, :], 1, 1
+                        )
+
+                    over_cols(model, cut, product)
+                with scope("calm"):
+                    pl.semaphore_wait(calm.at[h], lax.min(t, 1) + lax.min(nt - 1 - t, 1))
+                for s in which:
+                    inward.edge(s)
+
+            def gi_near(s):
+                with scope("b_near"):
+                    inward.relay(inward.near, s)
+
+            def gi_far(s):
+                with scope("b_far"):
+                    inward.relay(inward.far, s)
+
+            half_a, half_b = range(first_half), range(first_half, pieces)
+            pairs = queries // LANES
+            with scope("free0"):
+                free(s_gate, d_gate, 0)
+            with scope("b_give"):
+                pl.semaphore_wait(ready.at[0], width)
+                s_down.give()
+            br(3, 3)
+            gather_br.complete(range(pieces))
+            with scope("b_gm"):
+                loads[0].wait()
+                gm[...] = dot(branch[...], wo_v[...], 1, 1).astype(BF)
+            quiet(0)
+
+            @pl.loop(0, 2)
+            def _(h):
+                att(h * (pairs // 2), (h + 1) * (pairs // 2))
+
+                @pl.when(h == 0)
+                def _():
+                    y_near(2)
+                    with scope("b_take"):
+                        take(s_down)
+
+            y_near(3)
+            key = dkey[0] + pltpu.roll(dkey[1], HD, 1)
+            value = pltpu.roll(dval[0], HD, 1) + dval[1]
+            key = key * cos[...] - swapped(key) * sin[...]
+            dqkv[:, queries : queries + LANES] = jnp.where(
+                lane_index(key.shape) < HD, key, value
+            ).astype(BF)
+            loads[1].wait()
+            gi_part(0)
+            y_far(2)
+            with scope("ya_far"):
+                scatter_ya.relay(scatter_ya.far, 1)
+            y_far(3)
+            with scope("free1"):
+                freed(d_gate, 0).wait()
+                free(s_up, d_up, 1)
+            gi_near(0)
+            for s in half_b:
+                y_own(s)
+            scatter_y.finish(half_b)
+            quiet(1)
+            gi_part(1)
+            gi_far(0)
+            with scope("b_fill"):
+                loads[2].wait()
+                s_down.given()
+                pl.semaphore_wait(ready.at[1], width)
+                s_qkv.give()
+            gi_near(1)
+            with scope("b_fill"):
+                take(s_qkv)
+                s_out.give()
+            for s in half_a:
+                with scope("y_own"):
+                    block_ = slice(s * size, (s + 1) * size)
+                    scatter_ya.own_into(s, hid, block_)
+                    y[block_, :] = hid[block_, :].astype(BF)
+                    emit(y.at[pl.ds(s * size, size), :], y_o.at[pl.ds(s * size, size), :])
+            scatter_ya.finish(half_a)
+            with scope("b_done"):
+                for mask in range(1, nd):
+                    gain_copy(mask).wait_send()
+                cots.finish(range(pieces))
+                gather_br.finish(range(pieces))
+
+            def take_grad(s):
+                at = inward.own(s)
+                block = slice(s * size, (s + 1) * size)
+
+                def store(cols, value):
+                    gi[block, cols] += value
+
+                def store_gain(cols, value):
+                    gsum[0:1, cols] += value
+
+                back_through_norm(
+                    lambda c: x[block, c].astype(F32), lambda c: part[at, c], gall, 0, store, store_gain
+                )
+
+            fills = [
+                functools.partial(on, s, stage)
+                for stage in range(stages)
+                for s in (s_down, s_qkv, s_out)
+            ]
+            gi_far(1)
+            with scope("b_fill"):
+                take(s_out)
+            gi_near(2)
+            gi_far(2)
+            with scope("b_fill"):
+                fills.pop(0)()
+            gi_near(3)
+            gi_far(3)
+            freed(d_up, 1).wait()
+            with jax.named_scope("b_own"):
+                for s in range(pieces):
+                    take_grad(s)
+                    emit(gi.at[pl.ds(s * size, size), :], gi_o.at[pl.ds(s * size, size), :])
+                    if s == pieces - 2:
+                        for _ in range(2):
+                            fills.pop(0)()
+            with jax.named_scope("b_gains"):
+                fold = model // 4
+                for i in range(4):
+                    cols = slice(i * fold, (i + 1) * fold)
+                    zslots[t, 2 * i : 2 * i + 2, :] = gsum[0:2, cols]
+
+                def along(step):
+                    return remote(
+                        zslots.at[t], zslots.at[t], zsem.at[0, step], zsem.at[1, step],
+                        {"tensor": lax.rem(t + step, nt)},
                     )
 
-                over_cols(model, cut, product)
-            with scope("calm"):
-                pl.semaphore_wait(calm.at[h], lax.min(t, 1) + lax.min(nt - 1 - t, 1))
-            for s in which:
-                inward.edge(s)
-
-        def gi_near(s):
-            with scope("b_near"):
-                inward.relay(inward.near, s)
-
-        def gi_far(s):
-            with scope("b_far"):
-                inward.relay(inward.far, s)
-
-        half_a, half_b = range(first_half), range(first_half, pieces)
-        pairs = queries // LANES
-        with scope("b_gm"):
-            loads[0].wait()
-            gm[...] = dot(branch[...], wo_v[...], 1, 1).astype(BF)
-        for s in half_a:
-            y_own(s)
-        scatter_y.finish(half_a)
-        quiet(0)
-        with scope("add0"):
-            on(s_up, 0)
-        with scope("free0"):
-            copy_gate = free(s_gate, d_gate, 0)
-
-        @pl.loop(0, 2)
-        def _(h):
-            att(h * (pairs // 2), (h + 1) * (pairs // 2))
-
-            @pl.when(h == 0)
-            def _():
-                y_near(2)
-
-        with scope("b_give"):
-            pl.semaphore_wait(ready.at[0], width)
-            s_down.give()
-        y_near(3)
-        key = dkey[0] + pltpu.roll(dkey[1], HD, 1)
-        value = pltpu.roll(dval[0], HD, 1) + dval[1]
-        key = key * cos[...] - swapped(key) * sin[...]
-        dqkv[:, queries : queries + LANES] = jnp.where(
-            lane_index(key.shape) < HD, key, value
-        ).astype(BF)
-        loads[1].wait()
-        gi_part(0)
-        with scope("b_take"):
-            take(s_down)
-        y_far(2)
-        with scope("free1"):
-            copy_gate.wait()
-            copies = [free(s_up, d_up, 1)]
-        y_far(3)
-        gi_near(0)
-        with scope("b_fill"):
-            loads[2].wait()
-            s_down.given()
-            pl.semaphore_wait(ready.at[1], width)
-            s_qkv.give()
-        for s in half_b:
-            y_own(s)
-        scatter_y.finish(half_b)
-        quiet(1)
-        gi_part(1)
-        gi_far(0)
-        with scope("b_fill"):
-            take(s_qkv)
-        gi_near(1)
-        with scope("b_fill"):
-            s_out.give()
-
-        with scope("b_done"):
-            for mask in range(1, nd):
-                gain_copy(mask).wait_send()
-            cots.finish(range(pieces))
-            gather_br.finish(range(pieces))
-
-        def take_grad(s):
-            at = inward.own(s)
-            block = slice(s * size, (s + 1) * size)
-
-            def store(cols, value):
-                gi[block, cols] += value
-
-            def store_gain(cols, value):
-                gsum[0:1, cols] += value
-
-            back_through_norm(
-                lambda c: x[block, c].astype(F32), lambda c: part[at, c], gall, 0, store, store_gain
-            )
-
-        fills = [
-            functools.partial(on, s, stage)
-            for stage in range(stages)
-            for s in (s_down, s_qkv, s_out)
-        ]
-        gi_far(1)
-        with scope("b_fill"):
-            take(s_out)
-        gi_near(2)
-        gi_far(2)
-        with scope("b_fill"):
-            fills.pop(0)()
-        gi_near(3)
-        gi_far(3)
-        with jax.named_scope("b_own"):
-            for s in range(pieces):
-                take_grad(s)
-                emit(gi.at[pl.ds(s * size, size), :], gi_o.at[pl.ds(s * size, size), :])
-                if s < pieces - 1 and fills:
-                    fills.pop(0)()
-        with jax.named_scope("b_gains"):
-            zslots[t] = gsum[...]
-
-            def along(step):
-                return remote(
-                    zslots.at[t], zslots.at[t], zsem.at[0, step], zsem.at[1, step],
-                    {"tensor": lax.rem(t + step, nt)},
-                )
-
-            for step in range(1, nt):
-                along(step).start()
-        with jax.named_scope("b_gains"):
-            for step in range(1, nt):
-                slot = zslots.at[lax.rem(t + nt - step, nt)]
-                remote(
-                    slot, slot, zsem.at[0, step], zsem.at[1, step], {"tensor": lax.rem(t + step, nt)}
-                ).wait_recv()
-            gsum[...] = sum(zslots[i] for i in range(nt))
-
-            def across(mask):
-                peer = flip(me, mask, width)
-                return remote(
-                    gsum.at[:, pl.ds(pl.multiple_of(peer * shard, shard), shard)], dslots.at[me],
-                    dsem.at[0, mask], dsem.at[1, mask], {"dp": peer},
-                )
-
-            for mask in range(1, nd):
-                across(mask).start()
-            dslots[me] = gsum[:, pl.ds(pl.multiple_of(me * shard, shard), shard)]
-        with jax.named_scope("b_rest"):
-            for fill in fills:
-                fill()
-            for src, dst in ((d_wq, d_wq_o), (d_kv, d_kv_o), (d_wo, d_wo_o), (d_down, d_down_o)):
-                emit(src, dst)
-        with jax.named_scope("b_gains"):
-            for mask in range(1, nd):
-                peer = flip(me, mask, width)
-                slot = dslots.at[peer]
-                remote(slot, slot, dsem.at[0, mask], dsem.at[1, mask], {"dp": peer}).wait_recv()
-            gain_out[...] = sum(dslots[i] for i in range(nd))
-            emit(gain_out, gain_o)
-            for step in range(1, nt):
-                along(step).wait_send()
-            for mask in range(1, nd):
-                across(mask).wait_send()
-        with jax.named_scope("end"):
-            for s in (s_qkv, s_out):
-                s.given()
-            for s in (s_down, s_qkv, s_out):
-                s.drain()
-            inward.finish(range(pieces))
-            for copy in copies + emitted:
-                copy.wait()
+                for step in range(1, nt):
+                    along(step).start()
+            with jax.named_scope("b_gains"):
+                for step in range(1, nt):
+                    slot = zslots.at[lax.rem(t + nt - step, nt)]
+                    remote(
+                        slot, slot, zsem.at[0, step], zsem.at[1, step], {"tensor": lax.rem(t + step, nt)}
+                    ).wait_recv()
+                total = sum(zslots[i] for i in range(nt))
+                for i in range(4):
+                    gsum[0:2, i * fold : (i + 1) * fold] = total[2 * i : 2 * i + 2, :]
+
+                def across(mask):
+                    peer = flip(me, mask, width)
+                    return remote(
+                        gsum.at[:, pl.ds(pl.multiple_of(peer * shard, shard), shard)], dslots.at[me],
+                        dsem.at[0, mask], dsem.at[1, mask], {"dp": peer},
+                    )
+
+                for mask in range(1, nd):
+                    across(mask).start()
+                dslots[me] = gsum[:, pl.ds(pl.multiple_of(me * shard, shard), shard)]
+            with jax.named_scope("b_rest"):
+                for fill in fills:
+                    fill()
+                emit(stage_v.at[:, pl.ds(0, queries)], d_wq_o)
+                emit(part.at[pl.ds(0, queries), pl.ds(model, shard)], d_wo_o)
+                emit(d_kv, d_kv_o)
+                emit(d_down, d_down_o)
+            with jax.named_scope("b_gains"):
+                for mask in range(1, nd):
+                    peer = flip(me, mask, width)
+                    slot = dslots.at[peer]
+                    remote(slot, slot, dsem.at[0, mask], dsem.at[1, mask], {"dp": peer}).wait_recv()
+                gain_out[...] = sum(dslots[i] for i in range(nd))
+                emit(gain_out, gain_o)
+                for step in range(1, nt):
+                    along(step).wait_send()
+                for mask in range(1, nd):
+                    across(mask).wait_send()
+            with jax.named_scope("end"):
+                for s in (s_qkv, s_out):
+                    s.given()
+                for s in (s_down, s_qkv, s_out):
+                    s.drain()
+                inward.finish(range(pieces))
+                for copy in emitted:
+                    copy.wait()
+
+        pl.run_scoped(
+            rear,
+            pltpu.VMEM((tokens, tokens), F32),
+            pltpu.VMEM((2, tokens, LANES), BF),
+            pltpu.VMEM((2, tokens, LANES), BF),
+            pltpu.VMEM((2, tokens, LANES), F32),
+            pltpu.VMEM((2, tokens, LANES), F32),
+            pltpu.VMEM((nd // 2, shard, hidden), BF),
+        )
 
     pl.run_scoped(
-        rear,
-        pltpu.VMEM((tokens, tokens), F32),
-        pltpu.VMEM((2, tokens, LANES), BF),
-        pltpu.VMEM((2, tokens, LANES), BF),
-        pltpu.VMEM((2, tokens, LANES), F32),
-        pltpu.VMEM((2, tokens, LANES), F32),
-        pltpu.VMEM((nd // 2, shard, hidden), BF),
+        second_part, pltpu.VMEM((tokens // 2, model), BF), pltpu.VMEM((nt, rows // 2, model), BF)
     )
 
 
@@ -1387,19 +1428,18 @@
             pltpu.VMEM((model, hidden), BF),
             pltpu.VMEM((model, hidden), BF),
             pltpu.VMEM((hidden, model), BF),
-            pltpu.VMEM((max(tokens, 2 * shard), max(model, 3 * span)), F32),
+            pltpu.VMEM((max(tokens, queries), max(model + shard, 3 * span)), F32),
         ]
         + line_scratch(nt, rows, model)
         + [
+            pltpu.VMEM((nt + 1, rows // 2, model), BF),
             pltpu.VMEM((2, half, shard, hidden), BF),
             pltpu.VMEM((2, 2, half - 1, shard // 2, hidden), BF),
             pltpu.VMEM((shard, hidden), F32),
             pltpu.VMEM((rows, model), BF),
             pltpu.VMEM((rows, model), F32),
             pltpu.VMEM((8, shard), F32),
-            pltpu.VMEM((shard, queries), F32),
             pltpu.VMEM((LANES, shard), F32),
-            pltpu.VMEM((queries, shard), F32),
             pltpu.VMEM((hidden, shard), F32),
             pltpu.VMEM((shard, wide), BF),
             pltpu.VMEM((8, shard), F32),
@@ -1411,7 +1451,7 @@
             pltpu.VMEM((tokens, LANES), F32),
             pltpu.VMEM((tokens, LANES), F32),
             pltpu.VMEM((8, model), F32),
-            pltpu.VMEM((nt, 8, model), F32),
+            pltpu.VMEM((nt, 8, model // 4), F32),
             pltpu.VMEM((nd, 8, shard), F32),
             dma(2, nd),
             dma(7),
@@ -1419,6 +1459,7 @@
             dma(4, nt, PIECES),
             dma(4, nt, PIECES),
             dma(2, 2, nt, PIECES),
+            dma(2, 2, nt, PIECES // 2),
             dma(8, 2, half - 1),
             dma(8, 2, half - 1),
             dma(8, half),
@@ -1790,7 +1831,9 @@
         and w_query.shape[1] % LANES == 0
         and w_key.shape[1] == HD
         and segment_ids.shape[0] == nt * layer_input.shape[0]
-        and segment_ids.shape[0] % LANES == 0
+        and segment_ids.shape[0] % (8 * LANES // 2) == 0
+        and w_gate.shape[1] >= w_query.shape[1] + segment_ids.shape[0]
+        and layer_input.shape[1] >= 2 * segment_ids.shape[0]
     )
 
 

time: 270 us -> 267 us (0.989)
  Pallas kernels: 269 us -> 266 us
    pallas_call x1, Pallas kernels: 263 us -> 259 us  [layer(): pl.pallas_call(functools.partial(layer_kernel, nt, width), out_shape=[o f...]
where the time goes in v1:
time: 267 us
  Pallas kernels  266 us (100%)
    pallas_call x1, Pallas kernels, layer(): pl.pallas_call(functools.partial(layer_kernel, nt, width), out_shape=[o f...  259 us
    pallas_call x1, Pallas kernels, hand_over(): pl.pallas_call(functools.partial(hand_over_kernel, count, kv), out_shape=...  6.35 us

profile of v1, /device:TPU:0, one launch (start us, length us, event | category | flops | bytes accessed | tf_op | source)
XLA Modules:
  0.0 266.6 jit_solution(9925060635550952440)
XLA Ops:
  0.6 259.4 %layer.1 = (bf16[128,2048]{1,0:T(8,128)(2,1)}, f32[128,2048]{1,0:T(8,128)}, f32[8,256]{1,0:T(8,128)}, f32[256,512]{1,0:T(8,128)}, f32[128,256]{1,0:T(8,128)}, /*...) custom-call(bf16[128,2048]{1,0:T(8,128)(2,1)} %x.1, ...), custom_call_target="tpu_custom_call" | custom-call | tf_op jit(solution)/shard_map/layer/pallas_call | solution.py:1417
  260.0 6.4 %hand_over.1 = (bf16[128,2048]{1,0:T(8,128)(2,1)}, f32[128,2048]{1,0:T(8,128)}, f32[256,512]{1,0:T(8,128)}, f32[512,256]{1,0:T(8,128)}, f32[256,1408]{1,0:T(8,12...) custom-call(bf16[128,2048]{1,0:T(8,128)(2,1)} %get-tuple-element.31., ...), custom_call_target="tpu_custom_call" | custom-call | tf_op jit(solution)/shard_map/hand_over/pallas_call | solution.py:1517

commit v2 on v1

--- a/solution.py
+++ b/solution.py
@@ -369,6 +369,17 @@
             slot = self.slots - 1 - k
             self.sent[slot] = self.chunk(self.at(2 * slot + 1)).astype(BF)
             self.pair(slot).start()
+
+    def prepare(self):
+        @pl.loop(0, self.slots)
+        def _(k):
+            slot = self.slots - 1 - k
+            self.sent[slot] = self.chunk(self.at(2 * slot + 1)).astype(BF)
+
+    def dispatch(self):
+        @pl.loop(0, self.slots)
+        def _(k):
+            self.pair(self.slots - 1 - k).start()
 
     def given(self):
         @pl.loop(0, self.slots)
@@ -871,10 +882,23 @@
     gsum[...] = jnp.zeros_like(gsum)
     gather_br = LineGather(branch, natural, size, t, nt, line_sem)
 
-    def second_part(y_first, y_sent):
+    def second_part(y_first, y_sent, given):
         scatter_ya = LineScatter(y_first, shuffled, y_sent, y_arrived, t, nt, first_sem)
 
-        def feed(dg, du, given):
+        def freed(out, slot):
+            return pltpu.make_async_copy(stage_v, out, out_sem.at[1 + slot])
+
+        def free(s, out, slot):
+            s.add(stages - 1)
+            freed(out, slot).start()
+            s.drain()
+            for bit in range(width):
+                pl.semaphore_signal(
+                    ready.at[slot], inc=1, device_id={"dp": flip(me, 1 << bit, width)},
+                    device_id_type=pl.DeviceIdType.MESH,
+                )
+
+        def feed(dg, du):
             cuts = tiles_of(hidden, 6)
             span = max(width_ for _, width_ in cuts)
             half = tokens // 2
@@ -887,11 +911,15 @@
                 part[held, 0:width_] = dot(rowsbuf[mine, :], gate_v[:, at])
                 part[held, span : span + width_] = dot(rowsbuf[mine, :], up_v[:, at])
 
-            def tile_out(h, i):
+            def tile_down(h, i):
                 start, width_ = cuts[i]
                 at = slice(start, start + width_)
                 held = mine = slice(h * half, (h + 1) * half)
                 part[held, 2 * span : 2 * span + width_] = dot(cf[mine, :], down_v[at, :], 1, 1)
+
+            def tile_out(h, i):
+                start, width_ = cuts[i]
+                at = slice(start, start + width_)
 
                 @pl.loop(0, half // block)
                 def _(k):
@@ -909,6 +937,7 @@
             def tile(h, i):
                 with scope("tile"):
                     tile_in(h, i)
+                    tile_down(h, i)
                     tile_out(h, i)
 
             def back_dots(h):
@@ -1037,6 +1066,7 @@
                 g_down.place(place_sem.at[4]).wait()
                 g_down.pair_wait()
             with scope("tile"):
+                tile_down(0, 0)
                 tile_out(0, 0)
             o_take(3)
             nf(1, 2)
@@ -1062,12 +1092,16 @@
             nf(2, 3)
             gn_far(0)
             cot_steps(3, half_b)
+            cots.complete(half_b)
             gn_near(1)
+            with scope("tile"):
+                tile_down(1, 0)
             nf(3, 3)
             gather_nf.complete(half_b)
-            cots.complete(half_b)
             gather_nf.finish(half_a)
-            tile(1, 0)
+            with scope("tile"):
+                tile_in(1, 0)
+                tile_out(1, 0)
             gn_far(1)
             gn_take(0)
             for i in range(1, len(cuts)):
@@ -1092,16 +1126,23 @@
             br(1, 1)
             br(3, 0)
             with scope("gn_fill"):
-                take(s_up)
+                s_up.take()
             gn_near(3)
             gather_nf.finish(half_b)
             gn_take(2)
             scatter_ya.edge(1)
             gn_far(3)
             ya_near(0)
+            at_end = (t == 0) | (t == nt - 1)
+
+            def gate_on():
+                with scope("add0"):
+                    on(s_gate, 0)
+                    s_up.send(0)
+
+            pl.when(at_end)(gate_on)
             gn_take(3)
-            with scope("add0"):
-                on(s_gate, 0)
+            pl.when(jnp.logical_not(at_end))(gate_on)
             br(2, 1)
             br(1, 2)
             br(3, 1)
@@ -1112,19 +1153,21 @@
             scatter_gn.finish(half_b)
             scatter_y.edge(2)
             scatter_y.edge(3)
-            br(3, 2)
-            br(2, 3)
-            ya_near(1)
-            with scope("add0"):
-                on(s_up, 0)
+            with scope("b_give"):
+                s_up.given()
+                s_down.chunk, s_down.sent = chunk_of(cf, act), given
+                s_down.prepare()
+            with scope("free0"):
+                free(s_gate, d_gate, 0)
+            with scope("b_give"):
+                pl.semaphore_wait(ready.at[0], width)
+                s_down.dispatch()
             scatter_gn.finish(half_a)
-            s_up.given()
 
         pl.run_scoped(
             feed,
             pltpu.VMEM((tokens, hidden), BF),
             pltpu.VMEM((tokens, hidden), BF),
-            pltpu.VMEM((nd // 2, shard, hidden), BF),
         )
 
         wo_v = down_v.at[pl.ds(0, queries), :]
@@ -1133,7 +1176,7 @@
         gm = up_v.at[pl.ds(0, tokens), pl.ds(0, queries)]
         dqkv = up_v.at[pl.ds(tokens, tokens), pl.ds(0, wide)]
 
-        def rear(bias, kpad, vpad, dkey, dval, given):
+        def rear(bias, kpad, vpad, dkey, dval):
             inward = LineScatter(part, shuffled, sent, arrived, t, nt, sum_sem)
             for g in gathers:
                 g.drain()
@@ -1148,7 +1191,6 @@
             pad_pair(kvo[...].astype(F32), kpad, vpad)
             dkey[...] = jnp.zeros_like(dkey)
             dval[...] = jnp.zeros_like(dval)
-            s_down.chunk, s_down.sent = chunk_of(cf, act), given
             s_qkv.chunk, s_qkv.sent = chunk_of(na_v, dqkv), given.at[:, :, for_qkv]
             s_out.chunk, s_out.sent = chunk_of(branch, mo), given.at[:, :, for_wo]
 
@@ -1156,19 +1198,6 @@
                 with scope("b_att"):
                     attend_back_pairs(
                         first, last, qo, gm, mo, lo, kpad, vpad, bias, cos, sin, dqkv, dkey, dval
-                    )
-
-            def freed(out, slot):
-                return pltpu.make_async_copy(stage_v, out, out_sem.at[1 + slot])
-
-            def free(s, out, slot):
-                s.add(stages - 1)
-                freed(out, slot).start()
-                s.drain()
-                for bit in range(width):
-                    pl.semaphore_signal(
-                        ready.at[slot], inc=1, device_id={"dp": flip(me, 1 << bit, width)},
-                        device_id_type=pl.DeviceIdType.MESH,
                     )
 
             def quiet(h):
@@ -1210,11 +1239,14 @@
 
             half_a, half_b = range(first_half), range(first_half, pieces)
             pairs = queries // LANES
-            with scope("free0"):
-                free(s_gate, d_gate, 0)
-            with scope("b_give"):
-                pl.semaphore_wait(ready.at[0], width)
-                s_down.give()
+            br(3, 2)
+            br(2, 3)
+            scatter_ya.relay(scatter_ya.near, 1)
+            with scope("b_take"):
+                s_down.take()
+            with scope("add0"):
+                on(s_up, 0)
+                s_down.send(0)
             br(3, 3)
             gather_br.complete(range(pieces))
             with scope("b_gm"):
@@ -1229,8 +1261,6 @@
                 @pl.when(h == 0)
                 def _():
                     y_near(2)
-                    with scope("b_take"):
-                        take(s_down)
 
             y_near(3)
             key = dkey[0] + pltpu.roll(dkey[1], HD, 1)
@@ -1381,11 +1411,13 @@
             pltpu.VMEM((2, tokens, LANES), BF),
             pltpu.VMEM((2, tokens, LANES), F32),
             pltpu.VMEM((2, tokens, LANES), F32),
-            pltpu.VMEM((nd // 2, shard, hidden), BF),
         )
 
     pl.run_scoped(
-        second_part, pltpu.VMEM((tokens // 2, model), BF), pltpu.VMEM((nt, rows // 2, model), BF)
+        second_part,
+        pltpu.VMEM((tokens // 2, model), BF),
+        pltpu.VMEM((nt, rows // 2, model), BF),
+        pltpu.VMEM((nd // 2, shard, hidden), BF),
     )
 
 

time: 267 us -> 263 us (0.985)
  Pallas kernels: 266 us -> 262 us
    pallas_call x1, Pallas kernels: 259 us -> 255 us  [layer(): pl.pallas_call(functools.partial(layer_kernel, nt, width), out_shape=[o f...]
where the time goes in v2:
time: 263 us
  Pallas kernels  262 us (100%)
    pallas_call x1, Pallas kernels, layer(): pl.pallas_call(functools.partial(layer_kernel, nt, width), out_shape=[o f...  255 us
    pallas_call x1, Pallas kernels, hand_over(): pl.pallas_call(functools.partial(hand_over_kernel, count, kv), out_shape=...  6.35 us

profile of v2, /device:TPU:0, one launch (start us, length us, event | category | flops | bytes accessed | tf_op | source)
XLA Modules:
  0.0 262.6 jit_solution(7465689077870261280)
XLA Ops:
  0.6 255.5 %layer.1 = (bf16[128,2048]{1,0:T(8,128)(2,1)}, f32[128,2048]{1,0:T(8,128)}, f32[8,256]{1,0:T(8,128)}, f32[256,512]{1,0:T(8,128)}, f32[128,256]{1,0:T(8,128)}, /*...) custom-call(bf16[128,2048]{1,0:T(8,128)(2,1)} %x.1, ...), custom_call_target="tpu_custom_call" | custom-call | tf_op jit(solution)/shard_map/layer/pallas_call | solution.py:1449
  256.1 6.4 %hand_over.1 = (bf16[128,2048]{1,0:T(8,128)(2,1)}, f32[128,2048]{1,0:T(8,128)}, f32[256,512]{1,0:T(8,128)}, f32[512,256]{1,0:T(8,128)}, f32[256,1408]{1,0:T(8,12...) custom-call(bf16[128,2048]{1,0:T(8,128)(2,1)} %get-tuple-element.31., ...), custom_call_target="tpu_custom_call" | custom-call | tf_op jit(solution)/shard_map/hand_over/pallas_call | solution.py:1549
